TPU v7x, 32 devices: a whole 2x2x4 slice. The times are simulated.
32 devices in a mesh: rows: 8 (over z, y), basis: 4 (over x, core).
Axes of the slice: x: 2, y: 2, z: 4, core: 2. Of those that a mesh axis runs over, the one named last changes fastest.
Arguments:
- tiles: bfloat16 [2560, 256, 256], P(('rows', 'basis')), may hold values from 0 to 1
- tile_pairs: int32 [2560, 2], P(('rows', 'basis')), may hold values from 0 to 127, as said below
- degree: int32 [32768], P('rows'), may hold values from 848 to 5088, as said below
- start_block: float32 [32768, 128], P('rows'), may hold values from -8 to 8
- stored: float32 [16, 32768, 128], P('basis', 'rows'), may hold values from -6 to 6
Outputs:
- new_blocks: float32 [2, 32768, 128], P(None, 'rows')
- diagonal_blocks: float32 [2, 128, 128], replicated
- factors: float32 [2, 128, 128], replicated
Inputs may be any that keep to these rules, and one draw needn't show every extreme that they name: `tile_pairs`: tile t has its row block among the 16 blocks 16 * (t // 320) onward, and its column block within 32 blocks before or after that range of row blocks, cyclically over 128 blocks. `degree`: positive node degrees, given as an input and not equal to A's row sums; the stored blocks are not assumed orthonormal.
All inputs are finite; a program needn't handle non-finite values.
Results may differ from a plain program's by a relative error of at most 0.00076.
Values may be sent and summed in bfloat16 or wider, within the bound.
No kernel may reach another device: no remote copies, remote signals or barrier semaphores. Data moves between devices by JAX's collectives and lax.ppermute only.
A program may use at most 128 MiB of HBM per device.

v0:
```python
import jax
import jax.numpy as jnp
from jax import lax
from jax.sharding import PartitionSpec as P

ITERS = 2
REACH = 2


highest = lax.Precision.HIGHEST


def passed_along(shard, axis, by):
    length = lax.axis_size(axis)
    return lax.ppermute(shard, axis, [(i, (i + by) % length) for i in range(length)])


def neighbour_range(piece):
    pieces = []
    for distance in range(-REACH, REACH + 1):
        if distance == 0:
            pieces.append(piece)
        else:
            pieces.append(passed_along(piece, "rows", -distance))
    return jnp.concatenate(pieces, axis=0)


def local(tiles, tile_pairs, degree, start_block, stored):
    rows_count = lax.axis_size("rows")
    basis_count = lax.axis_size("basis")
    rows_index = lax.axis_index("rows")
    local_rows = start_block.shape[0]
    block_width = start_block.shape[1]
    tile_width = tiles.shape[1]
    blocks_here = local_rows // tile_width
    all_nodes = local_rows * rows_count
    all_blocks = blocks_here * rows_count
    row_scale = 1.0 / jnp.sqrt(degree.astype(jnp.float32))
    row_local = tile_pairs[:, 0] - rows_index * blocks_here
    column_local = jnp.mod(tile_pairs[:, 1] - (rows_index - REACH) * blocks_here, all_blocks)
    selector = (row_local[None, :] == jnp.arange(blocks_here, dtype=jnp.int32)[:, None]).astype(
        jnp.float32
    )
    current = start_block
    fresh = [start_block]
    block_list, diagonal_list, factor_list = ([], [], [])
    for iteration in range(ITERS):
        scaled = (row_scale[:, None] * current).astype(jnp.bfloat16)
        column_width = block_width // basis_count
        column_part = lax.dynamic_slice_in_dim(
            scaled, lax.axis_index("basis") * column_width, column_width, 1
        )
        extended = lax.all_gather(neighbour_range(column_part), "basis", axis=1, tiled=True)
        tile_grid = extended.reshape(-1, tile_width, block_width)
        chosen = jnp.take(tile_grid, column_local, axis=0)
        products = jnp.einsum("tij,tjc->tic", tiles, chosen, preferred_element_type=jnp.float32)
        partial_rows = jnp.dot(
            selector,
            products.reshape(products.shape[0], -1),
            precision=highest,
            preferred_element_type=jnp.float32,
        )
        image = lax.psum(partial_rows.reshape(local_rows, block_width), "basis")
        lifted = current - row_scale[:, None] * image
        fresh_stack = jnp.stack(fresh)
        stored_part = jnp.einsum("sri,rj->sij", stored, lifted, precision=highest)
        fresh_part = jnp.einsum("sri,rj->sij", fresh_stack, lifted, precision=highest)
        stored_coef, fresh_coef = lax.psum((stored_part, fresh_part), "rows")
        stored_coef = stored_coef / all_nodes
        fresh_coef = fresh_coef / all_nodes
        stored_term = jnp.einsum("sri,sij->rj", stored, stored_coef, precision=highest)
        correction = lax.psum(stored_term, "basis")
        remainder = lifted - correction
        remainder = remainder - jnp.einsum(
            "sri,sij->rj", fresh_stack, fresh_coef, precision=highest
        )
        gram_part = jnp.einsum("ri,rj->ij", remainder, remainder, precision=highest)
        gram = lax.psum(gram_part, "rows") / all_nodes
        lower = jnp.linalg.cholesky(gram)
        current = jax.scipy.linalg.solve_triangular(lower, remainder.T, lower=True).T
        fresh.append(current)
        block_list.append(current)
        diagonal_list.append(fresh_coef[-1])
        factor_list.append(lower.T)
    return (jnp.stack(block_list), jnp.stack(diagonal_list), jnp.stack(factor_list))


def solution(mesh):
    placed = (
        P(("rows", "basis"), None, None),
        P(("rows", "basis"), None),
        P("rows"),
        P("rows", None),
        P("basis", "rows", None),
    )
    return jax.shard_map(
        local,
        mesh=mesh,
        in_specs=placed,
        out_specs=(P(None, "rows", None), P(), P()),
        check_vma=False,
    )
```

profile of v0, /device:TPU:0, one launch (start us, length us, event | category | flops | bytes accessed | tf_op | source)
XLA Modules:
  0.0 890.0 jit_solution(16048043025722245657)
XLA Ops:
  33.9 39.9 %all-gather.3.cloned.1.call-done = bf16[20480,128]{0,1:T(8,128)(2,1)} async-done(((bf16[20480,32]{0,1:T(8,128)(2,1)}), bf16[20480,128]{0,1:T(8,128)(2,1)}) %all-gather.3.cloned.1.call-update) | async-done | bytes 5242896 | tf_op jit(solution)/shard_map/all_gather | solution.py:53
  90.1 15.4 %fusion.14 = f32[80,256,128]{1,2,0:T(8,128)} fusion(bf16[80,256,256]{2,1,0:T(8,128)(2,1)} %param.10, bf16[80,256,128]{2,1,0:T(8,128)(2,1)} %gather_fusion, pred[80]{0:T(512)(128)(4,1)S(1)} %get-tuple-element.16), kind=kOutput, calls=%fused_computation.23 | convolution fusion | flops 1344798720 | bytes 26214480 | tf_op jit(solution)/shard_map/tij,tjc->tic/dot_general | solution.py:56
  105.5 11.3 %copy.27 = f32[80,256,128]{2,1,0:T(8,128)} copy(f32[80,256,128]{1,2,0:T(8,128)} %fusion.14) | data formatting | bytes 20971520 | tf_op jit(solution)/shard_map/tij,tjc->tic/dot_general | solution.py:56
  116.8 13.3 %fusion.3 = f32[16,32768]{1,0:T(8,128)} fusion(f32[10,8,256,128]{3,2,1,0:T(8,128)} %bitcast.121, s32[80]{0:T(128)S(1)} %subtract_bitcast_fusion), kind=kOutput, calls=%fused_computation.5 | convolution fusion | flops 503317760 | bytes 12583232 | tf_op jit(solution)/shard_map/dot_general | solution.py:57
  136.0 51.3 %all-reduce.11.cloned.1.call-done = f32[4096,128]{0,1:T(8,128)} async-done(((f32[4096,128]{0,1:T(8,128)}), f32[4096,128]{0,1:T(8,128)}) %all-reduce.11.cloned.1.call-update) | async-done | bytes 2097168 | tf_op jit(solution)/shard_map/psum | solution.py:63
  200.2 71.7 %all-reduce.25.cloned.1.call-done = (f32[4,128,128]{1,2,0:T(8,128)}, f32[1,128,128]{1,2,0:T(8,128)}) async-done(((f32[4,128,128]{1,2,0:T(8,128)}, f32[1,128,128]{1,2,0:T(8,128)}), (f32[4,128,128]{1,2,0:T(8,128)}, f32[1,128,128]{1,2,0:T(8,128)})) %all-reduce.25.cloned.1.call-update) | async-done | bytes 327696 | tf_op jit(solution)/shard_map/psum | solution.py:68
  271.9 13.3 %convolution_bitcast_fusion.4 = f32[4096,128]{0,1:T(8,128)} fusion(f32[4,4096,128]{2,1,0:T(8,128)} %param.14, f32[4,128,128]{1,2,0:T(8,128)} %get-tuple-element.14), kind=kOutput, calls=%fused_computation.19 | convolution fusion | flops 3221291008 | bytes 10747904 | tf_op jit(solution)/shard_map/sri,sij->rj/dot_general | solution.py:71
  285.7 50.2 %all-reduce.13.cloned.1.call-done = f32[4096,128]{0,1:T(8,128)} async-done(((f32[4096,128]{0,1:T(8,128)}), f32[4096,128]{0,1:T(8,128)}) %all-reduce.13.cloned.1.call-update) | async-done | bytes 2097168 | tf_op jit(solution)/shard_map/psum | solution.py:72
  344.1 69.4 %all-reduce.15.cloned.1.call-done = f32[128,128]{0,1:T(8,128)} async-done(((f32[128,128]{0,1:T(8,128)}), f32[128,128]{0,1:T(8,128)}) %all-reduce.15.cloned.1.call-update) | async-done | bytes 65552 | tf_op jit(solution)/shard_map/psum | solution.py:78
  415.3 11.7 %cholesky.44 = f32[128,128]{1,0:T(8,128)S(1)} custom-call(f32[128,128]{1,0:T(8,128)S(1)} %fusion.46), custom_call_target="Cholesky" | custom-call | tf_op jit(solution)/shard_map/jit(cholesky)/cholesky | solution.py:79
  428.4 9.8 %custom-call.6 = f32[1,128,128]{1,2,0:T(8,128)S(1)} custom-call(f32[1,128,128]{2,1,0:T(8,128)S(1)} %get-tuple-element.19), custom_call_target="InvertDiagBlocksLowerTriangular" | custom-call | tf_op jit(solution)/shard_map/jit(_solve_triangular)/triangular_solve | solution.py:80
  462.4 39.6 %all-gather.5.cloned.1.call-done = bf16[20480,128]{0,1:T(8,128)(2,1)} async-done(((bf16[20480,32]{0,1:T(8,128)(2,1)}), bf16[20480,128]{0,1:T(8,128)(2,1)}) %all-gather.5.cloned.1.call-update) | async-done | bytes 5242896 | tf_op jit(solution)/shard_map/all_gather | solution.py:53
  510.1 8.3 gather_fusion.1
  518.4 15.4 %fusion.17 = f32[80,256,128]{1,2,0:T(8,128)} fusion(bf16[80,256,256]{2,1,0:T(8,128)(2,1)} %param.10, bf16[80,256,128]{2,1,0:T(8,128)(2,1)} %gather_fusion.1, pred[80]{0:T(512)(128)(4,1)S(1)} %copy-done.14), kind=kOutput, calls=%fused_computation.24 | convolution fusion | flops 1344798720 | bytes 26214480 | tf_op jit(solution)/shard_map/tij,tjc->tic/dot_general | solution.py:56
  533.8 11.3 %copy.34 = f32[80,256,128]{2,1,0:T(8,128)} copy(f32[80,256,128]{1,2,0:T(8,128)} %fusion.17) | data formatting | bytes 20971520 | tf_op jit(solution)/shard_map/tij,tjc->tic/dot_general | solution.py:56
  545.1 13.3 %fusion = f32[16,32768]{1,0:T(8,128)} fusion(f32[10,8,256,128]{3,2,1,0:T(8,128)} %bitcast.120, s32[80]{0:T(128)S(1)} %copy-done.16), kind=kOutput, calls=%fused_computation.2 | convolution fusion | flops 503317760 | bytes 12583232 | tf_op jit(solution)/shard_map/dot_general | solution.py:57
  564.3 51.3 %all-reduce.17.cloned.1.call-done = f32[4096,128]{0,1:T(8,128)} async-done(((f32[4096,128]{0,1:T(8,128)}), f32[4096,128]{0,1:T(8,128)}) %all-reduce.17.cloned.1.call-update) | async-done | bytes 2097168 | tf_op jit(solution)/shard_map/psum | solution.py:63
  617.4 8.6 fusion.34
  631.0 72.2 %all-reduce.23.cloned.1.call-done = (f32[4,128,128]{1,2,0:T(8,128)}, f32[2,128,128]{1,2,0:T(8,128)}) async-done(((f32[4,128,128]{1,2,0:T(8,128)}, f32[2,128,128]{1,2,0:T(8,128)}), (f32[4,128,128]{1,2,0:T(8,128)}, f32[2,128,128]{1,2,0:T(8,128)})) %all-reduce.23.cloned.1.call-update) | async-done | bytes 393232 | tf_op jit(solution)/shard_map/psum | solution.py:68
  703.2 13.3 %convolution_bitcast_fusion.2 = f32[4096,128]{0,1:T(8,128)} fusion(f32[4,4096,128]{2,1,0:T(8,128)} %param.14, f32[4,128,128]{1,2,0:T(8,128)} %get-tuple-element.12), kind=kOutput, calls=%fused_computation.16 | convolution fusion | flops 3221291008 | bytes 10747904 | tf_op jit(solution)/shard_map/sri,sij->rj/dot_general | solution.py:71
  717.5 49.7 %all-reduce.19.cloned.1.call-done = f32[4096,128]{0,1:T(8,128)} async-done(((f32[4096,128]{0,1:T(8,128)}), f32[4096,128]{0,1:T(8,128)}) %all-reduce.19.cloned.1.call-update) | async-done | bytes 2097168 | tf_op jit(solution)/shard_map/psum | solution.py:72
  777.3 68.7 %all-reduce.21.cloned.1.call-done = f32[128,128]{0,1:T(8,128)} async-done(((f32[128,128]{0,1:T(8,128)}), f32[128,128]{0,1:T(8,128)}) %all-reduce.21.cloned.1.call-update) | async-done | bytes 65552 | tf_op jit(solution)/shard_map/psum | solution.py:78
  847.8 11.7 %cholesky.55 = f32[128,128]{1,0:T(8,128)S(1)} custom-call(f32[128,128]{1,0:T(8,128)S(1)} %fusion.44), custom_call_target="Cholesky" | custom-call | tf_op jit(solution)/shard_map/jit(cholesky)/cholesky | solution.py:79
  861.6 9.8 %custom-call.7 = f32[1,128,128]{1,2,0:T(8,128)S(1)} custom-call(f32[1,128,128]{2,1,0:T(8,128)S(1)} %get-tuple-element.21), custom_call_target="InvertDiagBlocksLowerTriangular" | custom-call | tf_op jit(solution)/shard_map/jit(_solve_triangular)/triangular_solve | solution.py:80
  (128 shorter events, 144.5 us)
Async XLA Ops:
  7.2 66.6 %all-gather.3.cloned.1.call-start = ((), (), s32[]{:S(2)}) async-start(), calls=%async_computation | async-start | bytes 6553600 | tf_op jit(solution)/shard_map/all_gather | solution.py:53
  9.9 177.4 %copy-start = (f32[4096,128]{0,1:T(8,128)}, f32[4096,128]{0,1:T(8,128)S(1)}, u32[]{:S(2)}) copy-start(f32[4096,128]{0,1:T(8,128)S(1)} %copy.29) | copy-start | bytes 6291460
  9.9 12.3 %collective-permute-start = (bf16[4096,32]{0,1:T(8,128)(2,1)S(1)}, bf16[4096,32]{0,1:T(8,128)(2,1)S(1)}, u32[]{:S(2)}, u32[]{:S(2)}) collective-permute-start(bf16[4096,32]{0,1:T(8,128)(2,1)S(1)} %fusion.38), channel_id=1, source_target_pairs={{0,8},{4,12},{8,16},{12,20},{16,24},{20,28},{24,0},{28,4},{1,9},{5... | collective-permute-start | bytes 786440 | tf_op jit(solution)/shard_map/ppermute | solution.py:15
  13.0 16.1 %collective-permute-start.2 = (bf16[4096,32]{0,1:T(8,128)(2,1)S(1)}, bf16[4096,32]{0,1:T(8,128)(2,1)S(1)}, u32[]{:S(2)}, u32[]{:S(2)}) collective-permute-start(bf16[4096,32]{0,1:T(8,128)(2,1)S(1)} %fusion.38), channel_id=1, source_target_pairs={{0,28},{4,0},{8,4},{12,8},{16,12},{20,16},{24,20},{28,24},{1,29},{... | collective-permute-start | bytes 786440 | tf_op jit(solution)/shard_map/ppermute | solution.py:15
  16.2 12.8 %collective-permute-start.1 = (bf16[4096,32]{0,1:T(8,128)(2,1)S(1)}, bf16[4096,32]{0,1:T(8,128)(2,1)S(1)}, u32[]{:S(2)}, u32[]{:S(2)}) collective-permute-start(bf16[4096,32]{0,1:T(8,128)(2,1)S(1)} %fusion.38), channel_id=1, source_target_pairs={{0,4},{4,8},{8,12},{12,16},{16,20},{20,24},{24,28},{28,0},{1,5},{5... | collective-permute-start | bytes 786440 | tf_op jit(solution)/shard_map/ppermute | solution.py:15
  16.3 16.4 %collective-permute-start.3 = (bf16[4096,32]{0,1:T(8,128)(2,1)S(1)}, bf16[4096,32]{0,1:T(8,128)(2,1)S(1)}, u32[]{:S(2)}, u32[]{:S(2)}) collective-permute-start(bf16[4096,32]{0,1:T(8,128)(2,1)S(1)} %fusion.38), channel_id=1, source_target_pairs={{0,24},{4,28},{8,0},{12,4},{16,8},{20,12},{24,16},{28,20},{1,25},{... | collective-permute-start | bytes 786440 | tf_op jit(solution)/shard_map/ppermute | solution.py:15
  33.8 153.5 %all-reduce.11.cloned.1.call-start = ((), (), s32[]{:S(2)}) async-start(), calls=%async_computation.1 | async-start | bytes 4194304 | tf_op jit(solution)/shard_map/psum | solution.py:63
  33.8 56.2 %copy-start.13 = (pred[80]{0:T(512)(128)(4,1)}, pred[80]{0:T(512)(128)(4,1)S(1)}, u32[]{:S(2)}) copy-start(pred[80]{0:T(512)(128)(4,1)S(1)} %get-tuple-element.16) | copy-start | bytes 244
  33.9 48.0 %copy-start.12 = (s32[1024]{0:T(1024)}, s32[1024]{0:T(1024)S(1)}, u32[]{:S(2)}) copy-start(s32[1024]{0:T(1024)S(1)} %pad_clamp_fusion) | copy-start | bytes 12292
  33.9 82.9 %copy-start.15 = (s32[80]{0:T(128)}, s32[80]{0:T(128)S(1)}, u32[]{:S(2)}) copy-start(s32[80]{0:T(128)S(1)} %subtract_bitcast_fusion) | copy-start | bytes 964
  135.7 136.2 %all-reduce.25.cloned.1.call-start = ((), (), s32[]{:S(2)}) async-start(), calls=%async_computation.9 | async-start | bytes 655360 | tf_op jit(solution)/shard_map/psum | solution.py:68
  200.1 135.8 %all-reduce.13.cloned.1.call-start = ((), (), s32[]{:S(2)}) async-start(), calls=%async_computation.2 | async-start | bytes 4194304 | tf_op jit(solution)/shard_map/psum | solution.py:72
  271.9 64.0 %copy-start.11 = (f32[1,128,128]{1,2,0:T(8,128)S(1)}, f32[1,128,128]{1,2,0:T(8,128)}, u32[]{:S(2)}) copy-start(f32[1,128,128]{1,2,0:T(8,128)} %get-tuple-element.15) | copy-start | bytes 196612
  285.2 50.7 %copy-start.5 = (f32[4096,128]{0,1:T(8,128)S(1)}, f32[4096,128]{0,1:T(8,128)}, u32[]{:S(2)}) copy-start(f32[4096,128]{0,1:T(8,128)} %copy-done.4) | copy-start | bytes 6291460
  285.2 128.3 %all-reduce.15.cloned.1.call-start = ((), (), s32[]{:S(2)}) async-start(), calls=%async_computation.3 | async-start | bytes 131072 | tf_op jit(solution)/shard_map/psum | solution.py:78
  344.1 157.9 %all-gather.5.cloned.1.call-start = ((), (), s32[]{:S(2)}) async-start(), calls=%async_computation.4 | async-start | bytes 6553600 | tf_op jit(solution)/shard_map/all_gather | solution.py:53
  441.7 11.2 %collective-permute-start.4 = (bf16[4096,32]{0,1:T(8,128)(2,1)S(1)}, bf16[4096,32]{0,1:T(8,128)(2,1)S(1)}, u32[]{:S(2)}, u32[]{:S(2)}) collective-permute-start(bf16[4096,32]{0,1:T(8,128)(2,1)S(1)} %fusion.37), channel_id=1, source_target_pairs={{0,8},{4,12},{8,16},{12,20},{16,24},{20,28},{24,0},{28,4},{1,9},{5... | collective-permute-start | bytes 786440 | tf_op jit(solution)/shard_map/ppermute | solution.py:15
  443.7 15.0 %collective-permute-start.6 = (bf16[4096,32]{0,1:T(8,128)(2,1)S(1)}, bf16[4096,32]{0,1:T(8,128)(2,1)S(1)}, u32[]{:S(2)}, u32[]{:S(2)}) collective-permute-start(bf16[4096,32]{0,1:T(8,128)(2,1)S(1)} %fusion.37), channel_id=1, source_target_pairs={{0,28},{4,0},{8,4},{12,8},{16,12},{20,16},{24,20},{28,24},{1,29},{... | collective-permute-start | bytes 786440 | tf_op jit(solution)/shard_map/ppermute | solution.py:15
  446.7 11.9 %collective-permute-start.5 = (bf16[4096,32]{0,1:T(8,128)(2,1)S(1)}, bf16[4096,32]{0,1:T(8,128)(2,1)S(1)}, u32[]{:S(2)}, u32[]{:S(2)}) collective-permute-start(bf16[4096,32]{0,1:T(8,128)(2,1)S(1)} %fusion.37), channel_id=1, source_target_pairs={{0,4},{4,8},{8,12},{12,16},{16,20},{20,24},{24,28},{28,0},{1,5},{5... | collective-permute-start | bytes 786440 | tf_op jit(solution)/shard_map/ppermute | solution.py:15
  446.7 14.5 %collective-permute-start.7 = (bf16[4096,32]{0,1:T(8,128)(2,1)S(1)}, bf16[4096,32]{0,1:T(8,128)(2,1)S(1)}, u32[]{:S(2)}, u32[]{:S(2)}) collective-permute-start(bf16[4096,32]{0,1:T(8,128)(2,1)S(1)} %fusion.37), channel_id=1, source_target_pairs={{0,24},{4,28},{8,0},{12,4},{16,8},{20,12},{24,16},{28,20},{1,25},{... | collective-permute-start | bytes 786440 | tf_op jit(solution)/shard_map/ppermute | solution.py:15
  462.3 153.2 %all-reduce.17.cloned.1.call-start = ((), (), s32[]{:S(2)}) async-start(), calls=%async_computation.5 | async-start | bytes 4194304 | tf_op jit(solution)/shard_map/psum | solution.py:63
  564.0 139.3 %all-reduce.23.cloned.1.call-start = ((), (), s32[]{:S(2)}) async-start(), calls=%async_computation.8 | async-start | bytes 786432 | tf_op jit(solution)/shard_map/psum | solution.py:68
  630.9 136.2 %all-reduce.19.cloned.1.call-start = ((), (), s32[]{:S(2)}) async-start(), calls=%async_computation.6 | async-start | bytes 4194304 | tf_op jit(solution)/shard_map/psum | solution.py:72
  716.6 129.4 %all-reduce.21.cloned.1.call-start = ((), (), s32[]{:S(2)}) async-start(), calls=%async_computation.7 | async-start | bytes 131072 | tf_op jit(solution)/shard_map/psum | solution.py:78
  (12 other events, 71.5 us)
Sparse Core Ops, SparseCore 0:
  33.9 39.8 all-gather.2
  135.8 51.3 all-reduce.10
  200.2 71.6 all-reduce.24
  285.3 50.5 all-reduce.12
  344.2 69.3 all-reduce.14
  462.4 39.4 all-gather.4
  564.1 51.3 all-reduce.16
  631.1 72.1 all-reduce.22
  716.7 50.4 all-reduce.18
  776.6 69.3 all-reduce.20
where the time goes:
time: 899 us; the launch traced here: 890 us
  waiting for transfers between devices  592 us (66%)
  matrix products  130 us (14%)
  local copies, waits for them, and re-layouts  81.5 us (9%)
  other arithmetic  56.1 us (6%)
  starting transfers between devices  15.7 us (2%)
  between operations  15 us (2%)
    psum x2, waiting for transfers between devices, local(): stored_coef, fresh_coef = lax.psum((stored_part, fresh_part), 'rows')  144 us
    psum x2, waiting for transfers between devices, local(): gram = lax.psum(gram_part, 'rows') / all_nodes  138 us
    psum x2, waiting for transfers between devices, local(): image = lax.psum(partial_rows.reshape(local_rows, block_width), 'basis')  103 us
    psum x2, waiting for transfers between devices, local(): correction = lax.psum(stored_term, 'basis')  99.9 us
    all_gather x2, waiting for transfers between devices, local(): lax.all_gather(neighbour_range(column_part), 'basis', axis=1, tiled=True)  79.5 us
    dot_general x2, matrix products, local(): jnp.einsum('tij,tjc->tic', tiles, chosen, preferred_element_type=jnp.floa...  30.8 us
    ppermute x8, waiting for transfers between devices, passed_along(): lax.ppermute(shard, axis, [(i, (i + by) % length) for i in range(length)])  27.7 us
    dot_general x2, matrix products, local(): jnp.einsum('sri,sij->rj', stored, stored_coef, precision=highest)  26.6 us
  transfers between devices with their start and end apart: 18, of which 16 were waited for; matrix products, arithmetic and copies ran while one was open for 0% of the time, Pallas kernels for 0%

commit v1 on v0

v1 whole, which is shorter than its diff:
```python
import functools

import jax
import jax.numpy as jnp
from jax import lax
from jax.experimental import pallas as pl
from jax.experimental.pallas import tpu as pltpu
from jax.sharding import PartitionSpec as P

ITERS = 2
REACH = 2
PANEL = 16
CORE_BIT = 1
CHIP_BIT = 2

f32 = jnp.float32
bf16 = jnp.bfloat16
highest = lax.Precision.HIGHEST


def cost(flops, moved):
    return pl.CostEstimate(flops=int(flops), bytes_accessed=int(moved), transcendentals=0)


def halves_of(value):
    high = value.astype(bf16)
    return high, (value - high.astype(f32)).astype(bf16)


def product(left, right):
    return jnp.dot(left, right, preferred_element_type=f32)


def tile_kernel(
    step_tiles, place, row_ref, column_ref, tiles_ref, *refs
):
    pieces = len(place) * 2
    sources = refs[:pieces]
    keep_ref, send_ref, extended, total, arrived = refs[pieces:]
    half = keep_ref.shape[0]
    tile_width = tiles_ref.shape[1]
    core = lax.rem(lax.axis_index("basis"), 2)
    step = pl.program_id(0)

    @pl.when(step == 0)
    def _():
        copies = []
        for at, source in enumerate(sources):
            side = core if at % 2 == 0 else 1 - core
            begin = pl.multiple_of(place[at // 2] * 2 * half + side * half, half)
            copies.append(
                pltpu.make_async_copy(source, extended.at[pl.ds(begin, half)], arrived.at[at])
            )
        for copy in copies:
            copy.start()
        total[...] = jnp.zeros_like(total)
        for copy in copies:
            copy.wait()

    for at in range(step_tiles):
        row = row_ref[step * step_tiles + at]
        column = column_ref[step * step_tiles + at]
        block = extended[pl.ds(pl.multiple_of(column * tile_width, tile_width), tile_width), :]
        rows = pl.ds(pl.multiple_of(row * tile_width, tile_width), tile_width)
        total[rows, :] += product(tiles_ref[at], block)

    @pl.when(step == pl.num_programs(0) - 1)
    def _():
        keep_ref[...] = total[pl.ds(pl.multiple_of(core * half, half), half), :]
        send_ref[...] = total[pl.ds(pl.multiple_of((1 - core) * half, half), half), :]


def tile_products(tiles, row_local, column_local, place, sources):
    count, tile_width, _ = tiles.shape
    half, width = sources[0].shape
    step_tiles = 8 if count % 8 == 0 else 1
    return pl.pallas_call(
        functools.partial(tile_kernel, step_tiles, place),
        grid_spec=pltpu.PrefetchScalarGridSpec(
            num_scalar_prefetch=2,
            grid=(count // step_tiles,),
            in_specs=[pl.BlockSpec((step_tiles, tile_width, tile_width), lambda i, *_: (i, 0, 0))]
            + [pl.BlockSpec(memory_space=pl.ANY)] * len(sources),
            out_specs=[pl.BlockSpec((half, width), lambda i, *_: (0, 0))] * 2,
            scratch_shapes=[
                pltpu.VMEM((len(sources) * half, width), bf16),
                pltpu.VMEM((2 * half, width), f32),
                pltpu.SemaphoreType.DMA((len(sources),)),
            ],
        ),
        out_shape=[jax.ShapeDtypeStruct((half, width), f32)] * 2,
        cost_estimate=cost(2 * tiles.size * width, tiles.size * 2),
        name="tile_products",
    )(row_local, column_local, tiles, *sources)


def coefficient_kernel(fresh_count, has_before, place_ref, lifted_ref, stored_ref, *refs):
    fresh_refs = refs[:fresh_count]
    before_ref = refs[fresh_count] if has_before else None
    out_ref, left = refs[-2:]
    width = lifted_ref.shape[1]
    group = stored_ref.shape[0]
    step = pl.program_id(0)

    def put(columns, blocks):
        joined = jnp.concatenate(blocks, axis=1) if len(blocks) > 1 else blocks[0]
        high, low = halves_of(joined)
        sums = product(left[...], high) + product(left[...], low)
        sums = sums[:width, :] + sums[width:, :]
        out_ref[:, columns] = sums + before_ref[:, columns] if has_before else sums

    @pl.when(step == 0)
    def _():
        left[...] = jnp.concatenate(halves_of(lifted_ref[...].T), axis=0)

    begin = pl.multiple_of(step * group * width, width)
    put(pl.ds(begin, group * width), [stored_ref[at] for at in range(group)])

    @pl.when(step == pl.num_programs(0) - 1)
    def _():
        first = out_ref.shape[1] - fresh_count * width
        for at in range(0, fresh_count, 2):
            refs_here = fresh_refs[at : at + 2]
            put(pl.ds(first + at * width, len(refs_here) * width), [ref[...] for ref in refs_here])


def coefficients(lifted, stored, fresh, side, before):
    rows, width = lifted.shape
    count = stored.shape[0]
    group = 2 if count % 2 == 0 else 1
    columns = (count + len(fresh)) * width
    extra = [] if before is None else [before]
    whole = pl.BlockSpec((width, columns), lambda i, at: (0, 0))
    return pl.pallas_call(
        functools.partial(coefficient_kernel, len(fresh), before is not None),
        grid_spec=pltpu.PrefetchScalarGridSpec(
            num_scalar_prefetch=1,
            grid=(count // group,),
            in_specs=[
                pl.BlockSpec((rows, width), lambda i, at: (0, 0)),
                pl.BlockSpec((group, rows, width), lambda i, at: (i, at[0], 0)),
            ]
            + [pl.BlockSpec((rows, width), lambda i, at: (at[0], 0))] * len(fresh)
            + [whole] * len(extra),
            out_specs=whole,
            scratch_shapes=[pltpu.VMEM((2 * width, rows), bf16)],
        ),
        out_shape=jax.ShapeDtypeStruct((width, columns), f32),
        cost_estimate=cost(8 * rows * width * columns, 4 * rows * columns),
        name="coefficients",
    )(side, lifted, stored, *fresh, *extra)


def correction_kernel(place_ref, stored_ref, coefficient_ref, out_ref, right):
    count, _, width = stored_ref.shape

    @pl.when(pl.program_id(0) == 0)
    def _():
        for at in range(count):
            block = coefficient_ref[:, at * width : (at + 1) * width].T
            right[at * width : (at + 1) * width, :] = jnp.concatenate(halves_of(block), axis=1)

    sums = None
    for at in range(0, count, 2):
        pair = [stored_ref[i] for i in range(at, min(at + 2, count))]
        joined = jnp.concatenate(pair, axis=1) if len(pair) == 2 else pair[0]
        high, low = halves_of(joined)
        weights = right[at * width : (at + len(pair)) * width, :]
        term = product(high, weights) + product(low, weights)
        sums = term if sums is None else sums + term
    out_ref[...] = sums[:, :width] + sums[:, width:]


def correction(stored, coefficient, side):
    count, rows, width = stored.shape
    half = rows // 2
    step_rows = min(half, 512)
    steps = half // step_rows
    return pl.pallas_call(
        correction_kernel,
        grid_spec=pltpu.PrefetchScalarGridSpec(
            num_scalar_prefetch=1,
            grid=(steps,),
            in_specs=[
                pl.BlockSpec((count, step_rows, width), lambda i, at: (0, at[0] * steps + i, 0)),
                pl.BlockSpec((width, count * width), lambda i, at: (0, 0)),
            ],
            out_specs=pl.BlockSpec((step_rows, width), lambda i, at: (i, 0)),
            scratch_shapes=[pltpu.VMEM((count * width, 2 * width), bf16)],
        ),
        out_shape=jax.ShapeDtypeStruct((half, width), f32),
        cost_estimate=cost(8 * half * width * width * count, 4 * half * width * count),
        name="correction",
    )(side, stored, coefficient)


def remainder_kernel(first_column, place_ref, lifted_ref, keep_ref, near_ref, far_ref, coefficient_ref, *refs):
    fresh_refs = refs[:-2]
    out_ref, gram_ref = refs[-2:]
    width = out_ref.shape[1]
    value = lifted_ref[...] - ((keep_ref[...] + near_ref[...]) + far_ref[...])
    for at, ref in enumerate(fresh_refs):
        begin = first_column + at * width
        block = coefficient_ref[:, begin : begin + width]
        value = value - lax.dot_general(
            ref[...], block, (((1,), (1,)), ((), ())), precision=highest, preferred_element_type=f32
        )
    out_ref[...] = value
    gram_ref[...] = jnp.dot(value.T, value, precision=highest, preferred_element_type=f32)


def remainder_part(lifted, keep, near, far, coefficient, fresh, place, first_column):
    quarter, width = far.shape
    by_chip = pl.BlockSpec((quarter, width), lambda i, at: (at[0], 0))
    by_device = pl.BlockSpec((quarter, width), lambda i, at: (at[1], 0))
    here = pl.BlockSpec((quarter, width), lambda i, at: (0, 0))
    return pl.pallas_call(
        functools.partial(remainder_kernel, first_column),
        grid_spec=pltpu.PrefetchScalarGridSpec(
            num_scalar_prefetch=1,
            grid=(1,),
            in_specs=[by_chip, by_chip, by_chip, here]
            + [pl.BlockSpec(coefficient.shape, lambda i, at: (0, 0))]
            + [by_device] * len(fresh),
            out_specs=[here, pl.BlockSpec((width, width), lambda i, at: (0, 0))],
        ),
        out_shape=[
            jax.ShapeDtypeStruct((quarter, width), f32),
            jax.ShapeDtypeStruct((width, width), f32),
        ],
        cost_estimate=cost(12 * quarter * width * width * (len(fresh) + 1), 24 * quarter * width),
        name="remainder",
    )(place, lifted, keep, near, far, coefficient, *fresh)


def factor_kernel(gram_ref, upper_ref, inverse_ref, work):
    width = gram_ref.shape[0]
    row_at = lax.broadcasted_iota(jnp.int32, (width, width), 0)
    column_at = lax.broadcasted_iota(jnp.int32, (width, width), 1)
    work[:, :width] = gram_ref[...]
    work[:, width:] = (row_at == column_at).astype(f32)
    panel_row = lax.broadcasted_iota(jnp.int32, (PANEL, width), 0)
    panel_column = lax.broadcasted_iota(jnp.int32, (PANEL, width), 1)
    for begin in range(0, width, PANEL):
        end = begin + PANEL
        left = work[begin:end, :width]
        right = work[begin:end, width:]
        columns = [
            jnp.broadcast_to(left[:, begin + at : begin + at + 1], (PANEL, width)) for at in range(PANEL)
        ]
        for at in range(PANEL):
            scale = lax.rsqrt(columns[at][at : at + 1, :])
            column = columns[at] * scale
            below = jnp.where(panel_row > at, column, 0.0)
            left_row = left[at : at + 1, :] * scale
            right_row = right[at : at + 1, :] * scale
            left = jnp.where(panel_row == at, left_row, left - below * left_row)
            right = jnp.where(panel_row == at, right_row, right - below * right_row)
            for other in range(at + 1, PANEL):
                columns[other] = columns[other] - below * column[other : other + 1, :]
        left = jnp.where(panel_column >= panel_row + begin, left, 0.0)
        upper_ref[begin:end, :] = left
        inverse_ref[begin:end, :] = right
        if end < width:
            multipliers = left.T[end:, :]
            work[end:, :] -= jnp.dot(
                multipliers,
                jnp.concatenate([left, right], axis=1),
                precision=highest,
                preferred_element_type=f32,
            )


def factor(gram):
    width = gram.shape[0]
    return pl.pallas_call(
        factor_kernel,
        out_shape=[jax.ShapeDtypeStruct((width, width), f32)] * 2,
        scratch_shapes=[pltpu.VMEM((width, 2 * width), f32)],
        cost_estimate=cost(2e8, 4 * gram.size),
        name="factor",
    )(gram)


def solve_kernel(last, place_ref, inverse_ref, *refs):
    quarters = refs[:4]
    rest, right = refs[4:-1], refs[-1]
    step = pl.program_id(0)
    width = inverse_ref.shape[0]

    @pl.when(step == 0)
    def _():
        joined = jnp.concatenate(halves_of(inverse_ref[...].T), axis=1)
        right[...] = jnp.concatenate([joined, joined], axis=0)

    for at, ref in enumerate(quarters):

        @pl.when(step == at)
        def _():
            left = jnp.concatenate(halves_of(ref[...]), axis=1)
            sums = product(left, right[...])
            value = sums[:, :width] + sums[:, width:]
            if last:
                before_refs, out_ref = rest[:-1], rest[-1]
                for i, before in enumerate(before_refs):
                    out_ref[i] = before[...]
                out_ref[len(before_refs)] = value
            else:
                scale_ref, out_ref, mine_ref, other_ref = rest
                out_ref[...] = value
                target = mine_ref if at < 2 else other_ref
                quarter = ref.shape[0]
                begin = pl.multiple_of(lax.rem(place_ref[at], 2) * quarter, quarter)
                target[pl.ds(begin, quarter), :] = (scale_ref[...] * value).astype(bf16)


def solve(inverse, quarters, place, row_scale, before):
    quarter, width = quarters[0].shape
    last = before is not None
    here = pl.BlockSpec((quarter, width), lambda i, at: (0, 0))
    placed = pl.BlockSpec((quarter, width), lambda i, at: (at[i], 0))
    half = pl.BlockSpec((2 * quarter, width), lambda i, at: (0, 0))
    rows = 4 * quarter
    if last:
        extra = before
        out_specs = pl.BlockSpec((len(before) + 1, quarter, width), lambda i, at: (0, at[i], 0))
        out_shape = jax.ShapeDtypeStruct((len(before) + 1, rows, width), f32)
    else:
        extra = [row_scale]
        out_specs = [placed, half, half]
        out_shape = [jax.ShapeDtypeStruct((rows, width), f32)] + [
            jax.ShapeDtypeStruct((2 * quarter, width), bf16)
        ] * 2
    return pl.pallas_call(
        functools.partial(solve_kernel, last),
        grid_spec=pltpu.PrefetchScalarGridSpec(
            num_scalar_prefetch=1,
            grid=(4,),
            in_specs=[pl.BlockSpec((width, width), lambda i, at: (0, 0))] + [here] * 4 + [placed] * len(extra),
            out_specs=out_specs,
            scratch_shapes=[pltpu.VMEM((2 * width, 2 * width), bf16)],
        ),
        out_shape=out_shape,
        cost_estimate=cost(8 * rows * width * width, 12 * rows * width),
        name="solve",
    )(place, inverse, *quarters, *extra)


def along_rows(value, by):
    length = lax.axis_size("rows")
    return lax.ppermute(value, "rows", [(i, (i + by) % length) for i in range(length)])


def across(value, bit):
    return lax.ppermute(value, "basis", [(i, i ^ bit) for i in range(lax.axis_size("basis"))])


def summed(value, axes):
    rows, columns = value.shape
    devices = 1
    for axis in axes:
        devices *= lax.axis_size(axis)
    if rows % devices:
        return lax.psum(value, axes)
    pieces = value.reshape(devices, rows // devices, columns)
    taken = lax.all_to_all(pieces, axes, 0, 0, tiled=True)
    piece = jnp.sum(taken, axis=0)
    spread = jnp.broadcast_to(piece[None], pieces.shape)
    return lax.all_to_all(spread, axes, 0, 0, tiled=True).reshape(rows, columns)


def local(tiles, tile_pairs, degree, start_block, stored):
    rows_count = lax.axis_size("rows")
    rows_index = lax.axis_index("rows")
    basis_index = lax.axis_index("basis")
    core, chip = lax.rem(basis_index, 2), basis_index // 2
    local_rows, width = start_block.shape
    stored_here = stored.shape[0]
    half, quarter = local_rows // 2, local_rows // 4
    blocks_here = local_rows // tiles.shape[1]
    all_nodes = local_rows * rows_count
    all_blocks = blocks_here * rows_count
    row_local = tile_pairs[:, 0] - rows_index * blocks_here
    column_local = jnp.mod(tile_pairs[:, 1] - (rows_index - REACH) * blocks_here, all_blocks)
    row_scale = jnp.broadcast_to((1.0 / jnp.sqrt(degree.astype(f32)))[:, None], start_block.shape)

    def mine(value):
        return lax.dynamic_slice_in_dim(value, core * half, half, 0)

    def other(value):
        return lax.dynamic_slice_in_dim(value, (1 - core) * half, half, 0)

    side_mine = core.reshape(1)
    side_other = (1 - core).reshape(1)
    quarter_place = jnp.stack([chip, 2 * core + chip])
    solve_place = jnp.stack(
        [2 * core + chip, 2 * core + 1 - chip, 2 * (1 - core) + chip, 2 * (1 - core) + 1 - chip]
    )
    scaled = (row_scale * start_block).astype(bf16)
    scaled_mine, scaled_other = mine(scaled), other(scaled)
    scale_mine = mine(row_scale)
    distances = [distance for distance in range(-REACH, REACH + 1) if distance]
    current = start_block
    fresh = [start_block]
    diagonal_list, factor_list = ([], [])
    for iteration in range(ITERS):
        last = iteration == ITERS - 1
        got_mine = [along_rows(scaled_mine, -distance) for distance in distances]
        got_other = [across(value, CORE_BIT) for value in got_mine]
        place = [REACH] + [distance + REACH for distance in distances]
        sources = [scaled_mine, scaled_other]
        for pair in zip(got_mine, got_other):
            sources.extend(pair)
        keep, send = tile_products(tiles, row_local, column_local, place, sources)
        chip_sum = keep + across(send, CORE_BIT)
        image = chip_sum + across(chip_sum, CHIP_BIT)
        lifted = mine(current) - scale_mine * image
        lifted_other = across(lifted, CORE_BIT)
        part = coefficients(lifted, stored, fresh, side_mine, None)
        part = coefficients(lifted_other, stored, fresh, side_other, part)
        coefficient = summed(part, ("rows",)) / all_nodes
        stored_coefficient = coefficient[:, : stored_here * width]
        term_send = correction(stored, stored_coefficient, side_other)
        near = across(term_send, CORE_BIT)
        term_keep = correction(stored, stored_coefficient, side_mine)
        far = across(
            lax.dynamic_slice_in_dim(term_keep, (1 - chip) * quarter, quarter, 0)
            + lax.dynamic_slice_in_dim(near, (1 - chip) * quarter, quarter, 0),
            CHIP_BIT,
        )
        remainder, gram_part = remainder_part(
            lifted, term_keep, near, far, coefficient, fresh, quarter_place, stored_here * width
        )
        remainder_far = across(remainder, CHIP_BIT)
        quarters = [remainder, remainder_far, across(remainder, CORE_BIT), across(remainder_far, CORE_BIT)]
        gram = summed(gram_part, ("rows", "basis")) / all_nodes
        upper, inverse = factor(gram)
        diagonal_list.append(coefficient[:, -width:].T)
        factor_list.append(upper)
        if last:
            blocks = solve(inverse, quarters, solve_place, None, fresh[1:])
        else:
            current, scaled_mine, scaled_other = solve(inverse, quarters, solve_place, row_scale, None)
            fresh.append(current)
    return (blocks, jnp.stack(diagonal_list), jnp.stack(factor_list))


def solution(mesh):
    placed = (
        P(("rows", "basis"), None, None),
        P(("rows", "basis"), None),
        P("rows"),
        P("rows", None),
        P("basis", "rows", None),
    )
    return jax.shard_map(
        local,
        mesh=mesh,
        in_specs=placed,
        out_specs=(P(None, "rows", None), P(), P()),
        check_vma=False,
    )
```

time: 899 us -> 416 us (0.46)
  waiting for transfers between devices: 592 us -> 180 us
  matrix products: 130 us -> 0 us
  Pallas kernels: 0 us -> 104 us
  blocking collectives: 0 us -> 70.7 us
  local copies, waits for them, and re-layouts: 81.5 us -> 15.4 us
  other arithmetic: 56.1 us -> 14.3 us
  between operations: 15 us -> 1.05 us
  starting transfers between devices: 15.7 us -> 28.9 us
    psum x8 -> x0, waiting for transfers between devices: 485 us -> none  [the longest x2 144 us: local(): stored_coef, fresh_coef = lax.psum((stored_part, fresh_part), 'rows')]
    ppermute x8 -> x32, waiting for transfers between devices: 27.7 us -> 158 us  [the longest x24 94.2 us: across(): lax.ppermute(value, 'basis', [(i, i ^ bit) for i in range(lax.axis_size('...]
    dot_general x14 -> x0, matrix products: 123 us -> none  [the longest x2 30.8 us: local(): jnp.einsum('tij,tjc->tic', tiles, chosen, preferred_element_type=jnp.floa...]
    pallas_call x0 -> x16, Pallas kernels: none -> 104 us  [the longest x2 27.9 us: tile_products(): pl.pallas_call(functools.partial(tile_kernel, step_tiles, place), grid_sp...]
    all_gather x2 -> x0, waiting for transfers between devices: 79.5 us -> none  [local(): lax.all_gather(neighbour_range(column_part), 'basis', axis=1, tiled=True)]
    all_to_all x0 -> x5, blocking collectives: none -> 70.7 us  [the longest x3 42.8 us: summed(): taken = lax.all_to_all(pieces, axes, 0, 0, tiled=True)]
    another operation x13 -> x4, other arithmetic: 48 us -> 2.7 us  [the longest x2 1.52 us: local(): return (blocks, jnp.stack(diagonal_list), jnp.stack(factor_list))]
    reshape x6 -> x0, local copies, waits for them, and re-layouts: 27.4 us -> none  [the longest x2 16.2 us: local(): tile_grid = extended.reshape(-1, tile_width, block_width)]
  transfers between devices with their start and end apart: 18 -> 35, of which waited for: 16 -> 20; matrix products, arithmetic and copies ran while one was open for 0% -> 2% of each run, Pallas kernels for 0% -> 8%
where the time goes in v1:
time: 416 us; the launch traced here: 414 us
  waiting for transfers between devices  180 us (43%)
  Pallas kernels  104 us (25%)
  blocking collectives  70.7 us (17%)
  starting transfers between devices  28.9 us (7%)
  local copies, waits for them, and re-layouts  15.4 us (4%)
  other arithmetic  14.3 us (3%)
    ppermute x24, waiting for transfers between devices, across(): lax.ppermute(value, 'basis', [(i, i ^ bit) for i in range(lax.axis_size('...  94.2 us
    ppermute x8, waiting for transfers between devices, along_rows(): lax.ppermute(value, 'rows', [(i, (i + by) % length) for i in range(length)])  63.8 us
    all_to_all x3, blocking collectives, summed(): taken = lax.all_to_all(pieces, axes, 0, 0, tiled=True)  42.8 us
    pallas_call x2, Pallas kernels, tile_products(): pl.pallas_call(functools.partial(tile_kernel, step_tiles, place), grid_sp...  27.9 us
    all_to_all x2, blocking collectives, summed(): return lax.all_to_all(spread, axes, 0, 0, tiled=True).reshape(rows, columns)  27.9 us
    pallas_call x4, Pallas kernels, coefficients(): pl.pallas_call(functools.partial(coefficient_kernel, len(fresh), before i...  22.5 us
    pallas_call x4, Pallas kernels, correction(): pl.pallas_call(correction_kernel, grid_spec=pltpu.PrefetchScalarGridSpec(...  20.1 us
    pallas_call x2, Pallas kernels, solve(): pl.pallas_call(functools.partial(solve_kernel, last), grid_spec=pltpu.Pre...  12.3 us
  transfers between devices with their start and end apart: 35, of which 20 were waited for; matrix products, arithmetic and copies ran while one was open for 2% of the time, Pallas kernels for 8%

profile of v1, /device:TPU:0, one launch (start us, length us, event | category | flops | bytes accessed | tf_op | source)
XLA Modules:
  0.0 414.0 jit_solution(2535948470188272388)
XLA Ops:
  12.3 9.4 %collective-permute-done.6.refs_8_ = bf16[2048,128]{1,0:T(8,128)(2,1)S(1)} collective-permute-done((bf16[2048,128]{1,0:T(8,128)(2,1)S(1)}, bf16[2048,128]{1,0:T(8,128)(2,1)S(1)}, u32[]{:S(2)}, u32[]{:S(2)}) %collective-permute-start.6) | collective-permute-done | bytes 524320 | tf_op jit(solution)/shard_map/ppermute | solution.py:351
  21.7 11.4 %collective-permute-done.4.refs_6_ = bf16[2048,128]{1,0:T(8,128)(2,1)S(1)} collective-permute-done((bf16[2048,128]{1,0:T(8,128)(2,1)S(1)}, bf16[2048,128]{1,0:T(8,128)(2,1)S(1)}, u32[]{:S(2)}, u32[]{:S(2)}) %collective-permute-start.4) | collective-permute-done | bytes 524320 | tf_op jit(solution)/shard_map/ppermute | solution.py:351
  34.7 9.2 %collective-permute-done.refs_2_ = bf16[2048,128]{1,0:T(8,128)(2,1)S(1)} collective-permute-done((bf16[2048,128]{1,0:T(8,128)(2,1)S(1)}, bf16[2048,128]{1,0:T(8,128)(2,1)S(1)}, u32[]{:S(2)}, u32[]{:S(2)}) %collective-permute-start) | collective-permute-done | bytes 524320 | tf_op jit(solution)/shard_map/ppermute | solution.py:351
  46.0 14.0 %tile_products.2 = (f32[2048,128]{1,0:T(8,128)}, f32[2048,128]{1,0:T(8,128)}) custom-call(s32[80]{0:T(128)} %subtract_bitcast_fusion.row_ref, s32[80]{0:T(128)} %and_select_fusion.column_ref, bf16[80,256,256]{2,1,0:T(8,128)(2,1)} %tiles_ref.3, bf16[2048,128]{1,0:T(8,128)(2,1)} %copy-done.8, bf16[2048,128]{1,0:T(8,128)(2,1)} %get-tuple-element.36.refs_1_, ...), custom_call_target="tpu_custom_call" | custom-call | flops 1342177280 | bytes 10485760 | tf_op jit(solution)/shard_map/tile_products/pallas_call | solution.py:77
  65.8 23.9 %collective-permute-done.9 = f32[2048,128]{1,0:T(8,128)S(1)} collective-permute-done((f32[2048,128]{1,0:T(8,128)S(1)}, f32[2048,128]{1,0:T(8,128)S(1)}, u32[]{:S(2)}, u32[]{:S(2)}) %collective-permute-start.9) | collective-permute-done | bytes 1048608 | tf_op jit(solution)/shard_map/ppermute | solution.py:355
  102.9 15.7 %all_to_all.40 = f32[8,16,640]{2,1,0:T(8,128)S(1)} all-to-all(f32[8,16,640]{2,1,0:T(8,128)} %bitcast.36), channel_id=1, replica_groups=mesh['rows'=8,'basis'=4] {'rows'}, dimensions={0} | all-to-all | bytes 655360 | tf_op jit(solution)/shard_map/all_to_all | solution.py:366
  118.7 13.4 %all_to_all.41 = f32[8,16,640]{2,1,0:T(8,128)S(1)} all-to-all(f32[8,16,640]{2,1,0:T(8,128)S(1)} %broadcast_in_dim.14), channel_id=1, replica_groups=mesh['rows'=8,'basis'=4] {'rows'}, dimensions={0} | all-to-all | bytes 655360 | tf_op jit(solution)/shard_map/all_to_all | solution.py:369
  146.6 12.3 %collective-permute-done.12.far_ref = f32[1024,128]{1,0:T(8,128)S(1)} collective-permute-done((f32[1024,128]{1,0:T(8,128)S(1)}, f32[1024,128]{1,0:T(8,128)S(1)}, u32[]{:S(2)}, u32[]{:S(2)}) %collective-permute-start.12) | collective-permute-done | bytes 524320 | tf_op jit(solution)/shard_map/ppermute | solution.py:355
  166.2 12.2 %collective-permute-done.13.refs_1_ = f32[1024,128]{1,0:T(8,128)S(1)} collective-permute-done((f32[1024,128]{1,0:T(8,128)}, f32[1024,128]{1,0:T(8,128)S(1)}, u32[]{:S(2)}, u32[]{:S(2)}) %collective-permute-start.13) | collective-permute-done | bytes 524320 | tf_op jit(solution)/shard_map/ppermute | solution.py:355
  178.3 10.5 %all_to_all.42 = f32[32,4,128]{2,1,0:T(4,128)S(1)} all-to-all(f32[32,4,128]{2,1,0:T(4,128)} %bitcast.37), channel_id=1, replica_groups=mesh['rows'=8,'basis'=4] {'rows','basis'}, dimensions={0} | all-to-all | bytes 131072 | tf_op jit(solution)/shard_map/all_to_all | solution.py:366
  192.9 6.6 %all-to-all-done.3 = f32[32,4,128]{2,1,0:T(4,128)S(1)} async-done(((f32[32,4,128]{2,1,0:T(4,128)}), f32[32,4,128]{2,1,0:T(4,128)S(1)}, u32[]{:S(2)}, u32[]{:S(2)}) %all-to-all-start.3) | async-done | bytes 65568 | tf_op jit(solution)/shard_map/all_to_all | solution.py:369
  207.6 6.2 %solve.2 = (f32[4096,128]{1,0:T(8,128)}, bf16[2048,128]{1,0:T(8,128)(2,1)}, bf16[2048,128]{1,0:T(8,128)(2,1)}) custom-call(s32[4]{0:T(128)} %pad_add_fusion.place_ref, f32[128,128]{1,0:T(8,128)} %get-tuple-element.21.inverse_ref, f32[1024,128]{1,0:T(8,128)} %get-tuple-element.22.refs_0_, f32[1024,128]{1,0:T(8,128)} %copy-done.16, f32[1024,128]{1,0:T(8,128)} %copy-done.18, ...), custom_call_target="tpu_custom_call" | custom-call | flops 536870912 | bytes 6291456 | tf_op jit(solution)/shard_map/solve/pallas_call | solution.py:334
  217.8 11.0 %collective-permute-done.22.refs_8_ = bf16[2048,128]{1,0:T(8,128)(2,1)S(1)} collective-permute-done((bf16[2048,128]{1,0:T(8,128)(2,1)}, bf16[2048,128]{1,0:T(8,128)(2,1)S(1)}, u32[]{:S(2)}, u32[]{:S(2)}) %collective-permute-start.22) | collective-permute-done | bytes 524320 | tf_op jit(solution)/shard_map/ppermute | solution.py:351
  228.8 10.0 %collective-permute-done.20.refs_6_ = bf16[2048,128]{1,0:T(8,128)(2,1)S(1)} collective-permute-done((bf16[2048,128]{1,0:T(8,128)(2,1)}, bf16[2048,128]{1,0:T(8,128)(2,1)S(1)}, u32[]{:S(2)}, u32[]{:S(2)}) %collective-permute-start.20) | collective-permute-done | bytes 524320 | tf_op jit(solution)/shard_map/ppermute | solution.py:351
  240.1 9.9 %collective-permute-done.16.refs_2_ = bf16[2048,128]{1,0:T(8,128)(2,1)S(1)} collective-permute-done((bf16[2048,128]{1,0:T(8,128)(2,1)}, bf16[2048,128]{1,0:T(8,128)(2,1)S(1)}, u32[]{:S(2)}, u32[]{:S(2)}) %collective-permute-start.16) | collective-permute-done | bytes 524320 | tf_op jit(solution)/shard_map/ppermute | solution.py:351
  252.8 13.9 %tile_products.3 = (f32[2048,128]{1,0:T(8,128)}, f32[2048,128]{1,0:T(8,128)}) custom-call(s32[80]{0:T(128)} %subtract_bitcast_fusion.row_ref, s32[80]{0:T(128)} %and_select_fusion.column_ref, bf16[80,256,256]{2,1,0:T(8,128)(2,1)} %tiles_ref.3, bf16[2048,128]{1,0:T(8,128)(2,1)} %get-tuple-element.24.refs_0_, bf16[2048,128]{1,0:T(8,128)(2,1)} %get-tuple-element.25.refs_1_, ...), custom_call_target="tpu_custom_call" | custom-call | flops 1342177280 | bytes 10485760 | tf_op jit(solution)/shard_map/tile_products/pallas_call | solution.py:77
  272.1 24.2 %collective-permute-done.25 = f32[2048,128]{1,0:T(8,128)S(1)} collective-permute-done((f32[2048,128]{1,0:T(8,128)S(1)}, f32[2048,128]{1,0:T(8,128)S(1)}, u32[]{:S(2)}, u32[]{:S(2)}) %collective-permute-start.25) | collective-permute-done | bytes 1048608 | tf_op jit(solution)/shard_map/ppermute | solution.py:355
  297.6 5.7 %coefficients.6.refs_2_ = f32[128,768]{1,0:T(8,128)} custom-call(s32[1]{0:T(128)} %bitcast.7.place_ref, f32[2048,128]{1,0:T(8,128)} %copy-done.3, f32[4,4096,128]{2,1,0:T(8,128)} %stored_ref.15, f32[4096,128]{1,0:T(8,128)} %refs_0_.11, f32[4096,128]{1,0:T(8,128)} %get-tuple-element.23.refs_1_.refs_4_), custom_call_target="tpu_custom_call" | custom-call | flops 1610612736 | bytes 6291456 | tf_op jit(solution)/shard_map/coefficients/pallas_call | solution.py:134
  304.3 5.9 %coefficients.7 = f32[128,768]{1,0:T(8,128)} custom-call(s32[1]{0:T(128)} %bitcast.8.place_ref, f32[2048,128]{1,0:T(8,128)} %copy-done.10, f32[4,4096,128]{2,1,0:T(8,128)} %stored_ref.15, f32[4096,128]{1,0:T(8,128)} %refs_0_.11, f32[4096,128]{1,0:T(8,128)} %get-tuple-element.23.refs_1_.refs_4_, f32[128,768]{1,0:T(8,128)} %coefficients.6.refs_2_), custom_call_target="tpu_custom_call" | custom-call | flops 1610612736 | bytes 6291456 | tf_op jit(solution)/shard_map/coefficients/pallas_call | solution.py:134
  310.2 16.6 %all_to_all.43 = f32[8,16,768]{2,1,0:T(8,128)S(1)} all-to-all(f32[8,16,768]{2,1,0:T(8,128)} %bitcast.35), channel_id=1, replica_groups=mesh['rows'=8,'basis'=4] {'rows'}, dimensions={0} | all-to-all | bytes 786432 | tf_op jit(solution)/shard_map/all_to_all | solution.py:366
  326.8 14.5 %all_to_all.44 = f32[8,16,768]{2,1,0:T(8,128)S(1)} all-to-all(f32[8,16,768]{2,1,0:T(8,128)S(1)} %broadcast_in_dim.16), channel_id=1, replica_groups=mesh['rows'=8,'basis'=4] {'rows'}, dimensions={0} | all-to-all | bytes 786432 | tf_op jit(solution)/shard_map/all_to_all | solution.py:369
  354.5 13.6 %collective-permute-done.28.far_ref = f32[1024,128]{1,0:T(8,128)S(1)} collective-permute-done((f32[1024,128]{1,0:T(8,128)S(1)}, f32[1024,128]{1,0:T(8,128)S(1)}, u32[]{:S(2)}, u32[]{:S(2)}) %collective-permute-start.28) | collective-permute-done | bytes 524320 | tf_op jit(solution)/shard_map/ppermute | solution.py:355
  378.6 10.0 %all-to-all-done.6 = f32[32,4,128]{2,1,0:T(4,128)S(1)} async-done(((f32[32,4,128]{2,1,0:T(4,128)}), f32[32,4,128]{2,1,0:T(4,128)S(1)}, u32[]{:S(2)}, u32[]{:S(2)}) %all-to-all-start.6) | async-done | bytes 65568 | tf_op jit(solution)/shard_map/all_to_all | solution.py:366
  407.9 6.1 %solve.3 = f32[2,4096,128]{2,1,0:T(8,128)} custom-call(s32[4]{0:T(128)} %pad_add_fusion.place_ref, f32[128,128]{1,0:T(8,128)} %get-tuple-element.29.inverse_ref, f32[1024,128]{1,0:T(8,128)} %get-tuple-element.30.refs_0_, f32[1024,128]{1,0:T(8,128)} %copy-done.15, f32[1024,128]{1,0:T(8,128)} %copy-done.22, f32[1024,128]{1,0:T(8,128)} %copy-done.27, ...), custom_call_target="tpu_custom_call" | custom-call | flops 536870912 | bytes 6291456 | tf_op jit(solution)/shard_map/solve/pallas_call | solution.py:334
  (169 shorter events, 126.8 us)
Async XLA Ops:
  4.2 17.5 %collective-permute-start.6 = (bf16[2048,128]{1,0:T(8,128)(2,1)S(1)}, bf16[2048,128]{1,0:T(8,128)(2,1)S(1)}, u32[]{:S(2)}, u32[]{:S(2)}) collective-permute-start(bf16[2048,128]{1,0:T(8,128)(2,1)S(1)} %get-tuple-element.37.refs_0_), channel_id=1, source_target_pairs={{0,24},{4,28},{8,0},{12,4},{16,8},{20,12},{24,16},{28,20},{1,25},{... | collective-permute-start | bytes 1572872 | tf_op jit(solution)/shard_map/ppermute | solution.py:351
  9.3 23.8 %collective-permute-start.4 = (bf16[2048,128]{1,0:T(8,128)(2,1)S(1)}, bf16[2048,128]{1,0:T(8,128)(2,1)S(1)}, u32[]{:S(2)}, u32[]{:S(2)}) collective-permute-start(bf16[2048,128]{1,0:T(8,128)(2,1)S(1)} %get-tuple-element.37.refs_0_), channel_id=1, source_target_pairs={{0,28},{4,0},{8,4},{12,8},{16,12},{20,16},{24,20},{28,24},{1,29},{... | collective-permute-start | bytes 1572872 | tf_op jit(solution)/shard_map/ppermute | solution.py:351
  10.7 24.0 %collective-permute-start.2 = (bf16[2048,128]{1,0:T(8,128)(2,1)S(1)}, bf16[2048,128]{1,0:T(8,128)(2,1)S(1)}, u32[]{:S(2)}, u32[]{:S(2)}) collective-permute-start(bf16[2048,128]{1,0:T(8,128)(2,1)S(1)} %get-tuple-element.37.refs_0_), channel_id=1, source_target_pairs={{0,4},{4,8},{8,12},{12,16},{16,20},{20,24},{24,28},{28,0},{1,5},{5... | collective-permute-start | bytes 1572872 | tf_op jit(solution)/shard_map/ppermute | solution.py:351
  11.3 32.6 %collective-permute-start = (bf16[2048,128]{1,0:T(8,128)(2,1)S(1)}, bf16[2048,128]{1,0:T(8,128)(2,1)S(1)}, u32[]{:S(2)}, u32[]{:S(2)}) collective-permute-start(bf16[2048,128]{1,0:T(8,128)(2,1)S(1)} %get-tuple-element.37.refs_0_), channel_id=1, source_target_pairs={{0,8},{4,12},{8,16},{12,20},{16,24},{20,28},{24,0},{28,4},{1,9},{5... | collective-permute-start | bytes 1572872 | tf_op jit(solution)/shard_map/ppermute | solution.py:351
  21.7 23.4 %collective-permute-start.7 = (bf16[2048,128]{1,0:T(8,128)(2,1)S(1)}, bf16[2048,128]{1,0:T(8,128)(2,1)S(1)}, u32[]{:S(2)}, u32[]{:S(2)}) collective-permute-start(bf16[2048,128]{1,0:T(8,128)(2,1)S(1)} %collective-permute-done.6.refs_8_), channel_id=1, source_target_pairs={{0,1},{1,0},{2,3},{3,2},{4,5},{5,4},{6,7},{7,6},{8,9},{9,8},{10,11... | collective-permute-start | bytes 1572872 | tf_op jit(solution)/shard_map/ppermute | solution.py:355
  33.1 12.0 %collective-permute-start.5 = (bf16[2048,128]{1,0:T(8,128)(2,1)S(1)}, bf16[2048,128]{1,0:T(8,128)(2,1)}, u32[]{:S(2)}, u32[]{:S(2)}) collective-permute-start(bf16[2048,128]{1,0:T(8,128)(2,1)S(1)} %collective-permute-done.4.refs_6_), channel_id=1, source_target_pairs={{0,1},{1,0},{2,3},{3,2},{4,5},{5,4},{6,7},{7,6},{8,9},{9,8},{10,11... | collective-permute-start | bytes 1572872 | tf_op jit(solution)/shard_map/ppermute | solution.py:355
  34.7 10.4 %collective-permute-start.3 = (bf16[2048,128]{1,0:T(8,128)(2,1)S(1)}, bf16[2048,128]{1,0:T(8,128)(2,1)}, u32[]{:S(2)}, u32[]{:S(2)}) collective-permute-start(bf16[2048,128]{1,0:T(8,128)(2,1)S(1)} %collective-permute-done.2.refs_4_), channel_id=1, source_target_pairs={{0,1},{1,0},{2,3},{3,2},{4,5},{5,4},{6,7},{7,6},{8,9},{9,8},{10,11... | collective-permute-start | bytes 1572872 | tf_op jit(solution)/shard_map/ppermute | solution.py:355
  64.2 25.5 %collective-permute-start.9 = (f32[2048,128]{1,0:T(8,128)S(1)}, f32[2048,128]{1,0:T(8,128)S(1)}, u32[]{:S(2)}, u32[]{:S(2)}) collective-permute-start(f32[2048,128]{1,0:T(8,128)S(1)} %add.61), channel_id=1, source_target_pairs={{0,2},{1,3},{2,0},{3,1},{4,6},{5,7},{6,4},{7,5},{8,10},{9,11},{10,... | collective-permute-start | bytes 3145736 | tf_op jit(solution)/shard_map/ppermute | solution.py:355
  144.5 14.4 %collective-permute-start.12 = (f32[1024,128]{1,0:T(8,128)S(1)}, f32[1024,128]{1,0:T(8,128)S(1)}, u32[]{:S(2)}, u32[]{:S(2)}) collective-permute-start(f32[1024,128]{1,0:T(8,128)S(1)} %dynamic-slice_add_fusion.1), channel_id=1, source_target_pairs={{0,2},{1,3},{2,0},{3,1},{4,6},{5,7},{6,4},{7,5},{8,10},{9,11},{10,... | collective-permute-start | bytes 1572872 | tf_op jit(solution)/shard_map/ppermute | solution.py:355
  164.7 13.7 %collective-permute-start.13 = (f32[1024,128]{1,0:T(8,128)}, f32[1024,128]{1,0:T(8,128)S(1)}, u32[]{:S(2)}, u32[]{:S(2)}) collective-permute-start(f32[1024,128]{1,0:T(8,128)} %get-tuple-element.22.refs_0_), channel_id=1, source_target_pairs={{0,2},{1,3},{2,0},{3,1},{4,6},{5,7},{6,4},{7,5},{8,10},{9,11},{10,... | collective-permute-start | bytes 1572872 | tf_op jit(solution)/shard_map/ppermute | solution.py:355
  166.1 39.5 %collective-permute-start.14 = (f32[1024,128]{1,0:T(8,128)}, f32[1024,128]{1,0:T(8,128)S(1)}, u32[]{:S(2)}, u32[]{:S(2)}) collective-permute-start(f32[1024,128]{1,0:T(8,128)} %get-tuple-element.22.refs_0_), channel_id=1, source_target_pairs={{0,1},{1,0},{2,3},{3,2},{4,5},{5,4},{6,7},{7,6},{8,9},{9,8},{10,11... | collective-permute-start | bytes 1572872 | tf_op jit(solution)/shard_map/ppermute | solution.py:355
  178.3 27.3 %collective-permute-start.15 = (f32[1024,128]{1,0:T(8,128)S(1)}, f32[1024,128]{1,0:T(8,128)S(1)}, u32[]{:S(2)}, u32[]{:S(2)}) collective-permute-start(f32[1024,128]{1,0:T(8,128)S(1)} %collective-permute-done.13.refs_1_), channel_id=1, source_target_pairs={{0,1},{1,0},{2,3},{3,2},{4,5},{5,4},{6,7},{7,6},{8,9},{9,8},{10,11... | collective-permute-start | bytes 1572872 | tf_op jit(solution)/shard_map/ppermute | solution.py:355
  213.8 15.0 %collective-permute-start.22 = (bf16[2048,128]{1,0:T(8,128)(2,1)}, bf16[2048,128]{1,0:T(8,128)(2,1)S(1)}, u32[]{:S(2)}, u32[]{:S(2)}) collective-permute-start(bf16[2048,128]{1,0:T(8,128)(2,1)} %get-tuple-element.24.refs_0_), channel_id=1, source_target_pairs={{0,24},{4,28},{8,0},{12,4},{16,8},{20,12},{24,16},{28,20},{1,25},{... | collective-permute-start | bytes 1572872 | tf_op jit(solution)/shard_map/ppermute | solution.py:351
  214.6 24.2 %collective-permute-start.20 = (bf16[2048,128]{1,0:T(8,128)(2,1)}, bf16[2048,128]{1,0:T(8,128)(2,1)S(1)}, u32[]{:S(2)}, u32[]{:S(2)}) collective-permute-start(bf16[2048,128]{1,0:T(8,128)(2,1)} %get-tuple-element.24.refs_0_), channel_id=1, source_target_pairs={{0,28},{4,0},{8,4},{12,8},{16,12},{20,16},{24,20},{28,24},{1,29},{... | collective-permute-start | bytes 1572872 | tf_op jit(solution)/shard_map/ppermute | solution.py:351
  215.9 24.2 %collective-permute-start.18 = (bf16[2048,128]{1,0:T(8,128)(2,1)}, bf16[2048,128]{1,0:T(8,128)(2,1)S(1)}, u32[]{:S(2)}, u32[]{:S(2)}) collective-permute-start(bf16[2048,128]{1,0:T(8,128)(2,1)} %get-tuple-element.24.refs_0_), channel_id=1, source_target_pairs={{0,4},{4,8},{8,12},{12,16},{16,20},{20,24},{24,28},{28,0},{1,5},{5... | collective-permute-start | bytes 1572872 | tf_op jit(solution)/shard_map/ppermute | solution.py:351
  216.6 33.4 %collective-permute-start.16 = (bf16[2048,128]{1,0:T(8,128)(2,1)}, bf16[2048,128]{1,0:T(8,128)(2,1)S(1)}, u32[]{:S(2)}, u32[]{:S(2)}) collective-permute-start(bf16[2048,128]{1,0:T(8,128)(2,1)} %get-tuple-element.24.refs_0_), channel_id=1, source_target_pairs={{0,8},{4,12},{8,16},{12,20},{16,24},{20,28},{24,0},{28,4},{1,9},{5... | collective-permute-start | bytes 1572872 | tf_op jit(solution)/shard_map/ppermute | solution.py:351
  228.8 21.3 %collective-permute-start.23 = (bf16[2048,128]{1,0:T(8,128)(2,1)S(1)}, bf16[2048,128]{1,0:T(8,128)(2,1)S(1)}, u32[]{:S(2)}, u32[]{:S(2)}) collective-permute-start(bf16[2048,128]{1,0:T(8,128)(2,1)S(1)} %collective-permute-done.22.refs_8_), channel_id=1, source_target_pairs={{0,1},{1,0},{2,3},{3,2},{4,5},{5,4},{6,7},{7,6},{8,9},{9,8},{10,11... | collective-permute-start | bytes 1572872 | tf_op jit(solution)/shard_map/ppermute | solution.py:355
  238.7 11.3 %collective-permute-start.21 = (bf16[2048,128]{1,0:T(8,128)(2,1)S(1)}, bf16[2048,128]{1,0:T(8,128)(2,1)S(1)}, u32[]{:S(2)}, u32[]{:S(2)}) collective-permute-start(bf16[2048,128]{1,0:T(8,128)(2,1)S(1)} %collective-permute-done.20.refs_6_), channel_id=1, source_target_pairs={{0,1},{1,0},{2,3},{3,2},{4,5},{5,4},{6,7},{7,6},{8,9},{9,8},{10,11... | collective-permute-start | bytes 1572872 | tf_op jit(solution)/shard_map/ppermute | solution.py:355
  271.0 25.3 %collective-permute-start.25 = (f32[2048,128]{1,0:T(8,128)S(1)}, f32[2048,128]{1,0:T(8,128)S(1)}, u32[]{:S(2)}, u32[]{:S(2)}) collective-permute-start(f32[2048,128]{1,0:T(8,128)S(1)} %add.65), channel_id=1, source_target_pairs={{0,2},{1,3},{2,0},{3,1},{4,6},{5,7},{6,4},{7,5},{8,10},{9,11},{10,... | collective-permute-start | bytes 3145736 | tf_op jit(solution)/shard_map/ppermute | solution.py:355
  353.7 14.4 %collective-permute-start.28 = (f32[1024,128]{1,0:T(8,128)S(1)}, f32[1024,128]{1,0:T(8,128)S(1)}, u32[]{:S(2)}, u32[]{:S(2)}) collective-permute-start(f32[1024,128]{1,0:T(8,128)S(1)} %dynamic-slice_add_fusion), channel_id=1, source_target_pairs={{0,2},{1,3},{2,0},{3,1},{4,6},{5,7},{6,4},{7,5},{8,10},{9,11},{10,... | collective-permute-start | bytes 1572872 | tf_op jit(solution)/shard_map/ppermute | solution.py:355
  373.7 18.2 %collective-permute-start.29 = (f32[1024,128]{1,0:T(8,128)}, f32[1024,128]{1,0:T(8,128)S(1)}, u32[]{:S(2)}, u32[]{:S(2)}) collective-permute-start(f32[1024,128]{1,0:T(8,128)} %get-tuple-element.30.refs_0_), channel_id=1, source_target_pairs={{0,2},{1,3},{2,0},{3,1},{4,6},{5,7},{6,4},{7,5},{8,10},{9,11},{10,... | collective-permute-start | bytes 1572872 | tf_op jit(solution)/shard_map/ppermute | solution.py:355
  374.4 14.2 %all-to-all-start.6 = ((f32[32,4,128]{2,1,0:T(4,128)}), f32[32,4,128]{2,1,0:T(4,128)S(1)}, u32[]{:S(2)}, u32[]{:S(2)}) async-start(f32[32,4,128]{2,1,0:T(4,128)} %bitcast.38), calls=%async_computation.6 | async-start | bytes 131072 | tf_op jit(solution)/shard_map/all_to_all | solution.py:366
  378.5 28.4 %collective-permute-start.30 = (f32[1024,128]{1,0:T(8,128)}, f32[1024,128]{1,0:T(8,128)S(1)}, u32[]{:S(2)}, u32[]{:S(2)}) collective-permute-start(f32[1024,128]{1,0:T(8,128)} %get-tuple-element.30.refs_0_), channel_id=1, source_target_pairs={{0,1},{1,0},{2,3},{3,2},{4,5},{5,4},{6,7},{7,6},{8,9},{9,8},{10,11... | collective-permute-start | bytes 1572872 | tf_op jit(solution)/shard_map/ppermute | solution.py:355
  391.9 15.0 %collective-permute-start.31 = (f32[1024,128]{1,0:T(8,128)S(1)}, f32[1024,128]{1,0:T(8,128)S(1)}, u32[]{:S(2)}, u32[]{:S(2)}) collective-permute-start(f32[1024,128]{1,0:T(8,128)S(1)} %collective-permute-done.29.refs_1_), channel_id=1, source_target_pairs={{0,1},{1,0},{2,3},{3,2},{4,5},{5,4},{6,7},{7,6},{8,9},{9,8},{10,11... | collective-permute-start | bytes 1572872 | tf_op jit(solution)/shard_map/ppermute | solution.py:355
  (45 other events, 449.7 us)

commit v2 on v0

v2 whole, which is shorter than its diff:
```python
import functools

import jax
import jax.numpy as jnp
from jax import lax
from jax.experimental import pallas as pl
from jax.experimental.pallas import tpu as pltpu
from jax.sharding import PartitionSpec as P

ITERS = 2
REACH = 2
PANEL = 16
CORE_BIT = 1
CHIP_BIT = 2

f32 = jnp.float32
bf16 = jnp.bfloat16
highest = lax.Precision.HIGHEST


def cost(flops, moved):
    return pl.CostEstimate(flops=int(flops), bytes_accessed=int(moved), transcendentals=0)


def halves_of(value):
    high = value.astype(bf16)
    return high, (value - high.astype(f32)).astype(bf16)


def product(left, right):
    return jnp.dot(left, right, preferred_element_type=f32)


def quarter_places():
    basis_index = lax.axis_index("basis")
    core, chip = lax.rem(basis_index, 2), basis_index // 2
    return [2 * core + chip, 2 * core + 1 - chip, 2 * (1 - core) + chip, 2 * (1 - core) + 1 - chip]


def tile_kernel(step_tiles, targets, row_ref, column_ref, tiles_ref, *refs):
    pieces = len(targets)
    sources = refs[:pieces]
    outs = refs[pieces : pieces + 2]
    extended, total, arrived = refs[pieces + 2 :]
    quarter = outs[0].shape[0] // 2
    count, tile_width, _ = tiles_ref.shape
    places = quarter_places()
    copies = []
    for source, (at, index, which) in zip(sources, targets):
        begin = pl.multiple_of((at * 4 + places[which]) * quarter, quarter)
        copies.append(
            pltpu.make_async_copy(
                source.at[pl.ds(index * quarter, quarter)],
                extended.at[pl.ds(begin, quarter)],
                arrived.at[len(copies)],
            )
        )
    for copy in copies:
        copy.start()

    total[...] = jnp.zeros_like(total)
    for copy in copies:
        copy.wait()

    def visit(step, carry):
        for at in range(step_tiles):
            tile = step * step_tiles + at
            column = pl.multiple_of(column_ref[tile] * tile_width, tile_width)
            rows = pl.ds(pl.multiple_of(row_ref[tile] * tile_width, tile_width), tile_width)
            total[rows, :] += product(tiles_ref[tile], extended[pl.ds(column, tile_width), :])
        return carry

    lax.fori_loop(0, count // step_tiles, visit, 0)
    for at, place in enumerate(places):
        begin = at % 2 * quarter
        rows = pl.ds(pl.multiple_of(place * quarter, quarter), quarter)
        outs[at // 2][begin : begin + quarter, :] = total[rows, :]


def in_vmem(count):
    return [pl.BlockSpec(memory_space=pltpu.VMEM)] * count


def limits(mib):
    return pltpu.CompilerParams(vmem_limit_bytes=mib << 20)


def tile_products(tiles, row_local, column_local, ranges, sources):
    count = tiles.shape[0]
    width = sources[0][0][0].shape[1]
    quarter = sources[0][0][0].shape[0]
    step_tiles = 8 if count % 8 == 0 else 1
    targets, arrays = [], []
    for at, sides in zip(ranges, sources):
        for side, parts in enumerate(sides):
            for which in range(2):
                index = which if len(parts) == 1 else 0
                targets.append((at, index, 2 * side + which))
                arrays.append(parts[0] if len(parts) == 1 else parts[which])
    sources = arrays
    return pl.pallas_call(
        functools.partial(tile_kernel, step_tiles, targets),
        in_specs=[pl.BlockSpec(memory_space=pltpu.SMEM)] * 2
        + in_vmem(1)
        + [pl.BlockSpec(memory_space=pltpu.HBM)] * len(sources),
        out_specs=in_vmem(2),
        scratch_shapes=[
            pltpu.VMEM((len(sources) * quarter, width), bf16),
            pltpu.VMEM((4 * quarter, width), f32),
            pltpu.SemaphoreType.DMA((len(sources),)),
        ],
        out_shape=[jax.ShapeDtypeStruct((2 * quarter, width), f32)] * 2,
        compiler_params=limits(28),
        cost_estimate=cost(2 * tiles.size * width, tiles.size * 2),
        name="tile_products",
    )(row_local, column_local, tiles, *sources)


def coefficient_kernel(which, fresh_count, has_before, lifted_ref, stored_ref, *refs):
    fresh_refs = refs[: 2 * fresh_count]
    before_ref = refs[2 * fresh_count] if has_before else None
    out_ref = refs[-1]
    width = lifted_ref.shape[1]
    quarter = lifted_ref.shape[0] // 2
    left = jnp.concatenate(halves_of(lifted_ref[...].T), axis=0)
    blocks_count = stored_ref.shape[0] + fresh_count

    def take(at, side):
        if at < stored_ref.shape[0]:
            begin = quarter_places()[which[side]] * quarter
            return stored_ref[at, pl.ds(pl.multiple_of(begin, quarter), quarter), :]
        return fresh_refs[2 * (at - stored_ref.shape[0]) + side][...]

    for at in range(0, blocks_count, 2):
        pair = range(at, min(at + 2, blocks_count))
        sums = None
        for side in range(2):
            blocks = [take(i, side) for i in pair]
            joined = jnp.concatenate(blocks, axis=1) if len(blocks) > 1 else blocks[0]
            high, low = halves_of(joined)
            part = left[:, side * quarter : (side + 1) * quarter]
            term = product(part, high) + product(part, low)
            sums = term if sums is None else sums + term
        sums = sums[:width, :] + sums[width:, :]
        columns = slice(at * width, (at + len(pair)) * width)
        out_ref[:, columns] = sums + before_ref[:, columns] if has_before else sums


def coefficients(which, lifted, stored, fresh, before):
    half, width = lifted.shape
    columns = (stored.shape[0] + len(fresh)) * width
    extra = [] if before is None else [before]
    pieces = [block[at] for block in fresh for at in which]
    return pl.pallas_call(
        functools.partial(coefficient_kernel, which, len(fresh), before is not None),
        in_specs=in_vmem(2 + len(pieces) + len(extra)),
        out_specs=in_vmem(1)[0],
        out_shape=jax.ShapeDtypeStruct((width, columns), f32),
        compiler_params=limits(24),
        cost_estimate=cost(8 * half * width * columns, 4 * half * columns),
        name="coefficients",
    )(lifted, stored, *pieces, *extra)


def correction_kernel(which, stored_ref, coefficient_ref, *outs):
    count, _, width = stored_ref.shape
    quarter = outs[0].shape[0]
    step_rows = min(quarter, 512)
    weights = []
    for at in range(0, count, 2):
        blocks = [coefficient_ref[:, i * width : (i + 1) * width].T for i in range(at, min(at + 2, count))]
        joined = jnp.concatenate(blocks, axis=0) if len(blocks) > 1 else blocks[0]
        weights.append(jnp.concatenate(halves_of(joined), axis=1))
    for target, out_ref in zip(which, outs):
        begin = quarter_places()[target] * quarter
        for step in range(0, quarter, step_rows):
            rows = pl.ds(pl.multiple_of(begin + step, step_rows), step_rows)
            sums = None
            for at, weight in zip(range(0, count, 2), weights):
                blocks = [stored_ref[i, rows, :] for i in range(at, min(at + 2, count))]
                joined = jnp.concatenate(blocks, axis=1) if len(blocks) > 1 else blocks[0]
                high, low = halves_of(joined)
                term = product(high, weight) + product(low, weight)
                sums = term if sums is None else sums + term
            out_ref[step : step + step_rows, :] = sums[:, :width] + sums[:, width:]


def correction(which, stored, coefficient):
    count, rows, width = stored.shape
    quarter = rows // 4
    return pl.pallas_call(
        functools.partial(correction_kernel, which),
        in_specs=in_vmem(2),
        out_specs=in_vmem(len(which)),
        out_shape=[jax.ShapeDtypeStruct((quarter, width), f32)] * len(which),
        compiler_params=limits(24),
        cost_estimate=cost(8 * quarter * width * width * count * len(which), 4 * quarter * width * count),
        name="correction",
    )(stored, coefficient)


def remainder_kernel(first_column, lifted_ref, keep_ref, near_ref, far_ref, coefficient_ref, *refs):
    fresh_refs = refs[:-2]
    out_ref, gram_ref = refs[-2:]
    width = out_ref.shape[1]
    value = lifted_ref[...] - ((keep_ref[...] + near_ref[...]) + far_ref[...])
    for at, ref in enumerate(fresh_refs):
        begin = first_column + at * width
        block = coefficient_ref[:, begin : begin + width]
        value = value - lax.dot_general(
            ref[...], block, (((1,), (1,)), ((), ())), precision=highest, preferred_element_type=f32
        )
    out_ref[...] = value
    gram_ref[...] = jnp.dot(value.T, value, precision=highest, preferred_element_type=f32)


def remainder_part(lifted, keep, near, far, coefficient, fresh, first_column):
    quarter, width = far.shape
    return pl.pallas_call(
        functools.partial(remainder_kernel, first_column),
        in_specs=in_vmem(5 + len(fresh)),
        out_specs=in_vmem(2),
        out_shape=[
            jax.ShapeDtypeStruct((quarter, width), f32),
            jax.ShapeDtypeStruct((width, width), f32),
        ],
        compiler_params=limits(16),
        cost_estimate=cost(12 * quarter * width * width * (len(fresh) + 1), 24 * quarter * width),
        name="remainder",
    )(lifted, keep, near, far, coefficient, *fresh)


def factor_kernel(gram_ref, upper_ref, inverse_ref, work):
    width = gram_ref.shape[0]
    row_at = lax.broadcasted_iota(jnp.int32, (width, width), 0)
    column_at = lax.broadcasted_iota(jnp.int32, (width, width), 1)
    work[:, :width] = gram_ref[...]
    work[:, width:] = (row_at == column_at).astype(f32)
    panel_row = lax.broadcasted_iota(jnp.int32, (PANEL, width), 0)
    panel_column = lax.broadcasted_iota(jnp.int32, (PANEL, width), 1)
    for begin in range(0, width, PANEL):
        end = begin + PANEL
        left = work[begin:end, :width]
        right = work[begin:end, width:]
        columns = [
            jnp.broadcast_to(left[:, begin + at : begin + at + 1], (PANEL, width)) for at in range(PANEL)
        ]
        for at in range(PANEL):
            scale = lax.rsqrt(columns[at][at : at + 1, :])
            column = columns[at] * scale
            below = jnp.where(panel_row > at, column, 0.0)
            left_row = left[at : at + 1, :] * scale
            right_row = right[at : at + 1, :] * scale
            left = jnp.where(panel_row == at, left_row, left - below * left_row)
            right = jnp.where(panel_row == at, right_row, right - below * right_row)
            for other in range(at + 1, PANEL):
                columns[other] = columns[other] - below * column[other : other + 1, :]
        left = jnp.where(panel_column >= panel_row + begin, left, 0.0)
        upper_ref[begin:end, :] = left
        inverse_ref[begin:end, :] = right
        if end < width:
            multipliers = left.T[end:, :]
            work[end:, :] -= jnp.dot(
                multipliers,
                jnp.concatenate([left, right], axis=1),
                precision=highest,
                preferred_element_type=f32,
            )


def factor(gram):
    width = gram.shape[0]
    return pl.pallas_call(
        factor_kernel,
        out_shape=[jax.ShapeDtypeStruct((width, width), f32)] * 2,
        scratch_shapes=[pltpu.VMEM((width, 2 * width), f32)],
        compiler_params=limits(8),
        cost_estimate=cost(2e8, 4 * gram.size),
        name="factor",
    )(gram)


def solve_kernel(count, inverse_ref, *refs):
    joined = jnp.concatenate(halves_of(inverse_ref[...].T), axis=1)
    right = jnp.concatenate([joined, joined], axis=0)
    width = inverse_ref.shape[0]
    for at in range(count):
        value_ref, scale_ref, out_ref, scaled_ref = refs[at::count]
        left = jnp.concatenate(halves_of(value_ref[...]), axis=1)
        sums = product(left, right)
        value = sums[:, :width] + sums[:, width:]
        out_ref[...] = value
        scaled_ref[...] = (scale_ref[...] * value).astype(bf16)


def solve(inverse, values, scales):
    count = len(values)
    quarter, width = values[0].shape
    outs = pl.pallas_call(
        functools.partial(solve_kernel, count),
        in_specs=in_vmem(1 + 2 * count),
        out_specs=in_vmem(2 * count),
        out_shape=[jax.ShapeDtypeStruct((quarter, width), f32)] * count
        + [jax.ShapeDtypeStruct((quarter, width), bf16)] * count,
        compiler_params=limits(16),
        cost_estimate=cost(8 * count * quarter * width * width, 12 * count * quarter * width),
        name="solve",
    )(inverse, *values, *scales)
    return outs[:count], outs[count:]


def put_kernel(place_ref, *refs):
    out_ref = refs[-1]
    for at in range(4):

        @pl.when(pl.program_id(0) == at)
        def _():
            for i, ref in enumerate(refs[at:-1:4]):
                out_ref[i] = ref[...]


def put(place, blocks, total):
    quarter, width = blocks[0][0].shape
    flat = [block for quarters in blocks for block in quarters]
    return pl.pallas_call(
        put_kernel,
        grid_spec=pltpu.PrefetchScalarGridSpec(
            num_scalar_prefetch=1,
            grid=(4,),
            in_specs=[pl.BlockSpec((quarter, width), lambda i, at: (0, 0))] * len(flat),
            out_specs=pl.BlockSpec((len(blocks), quarter, width), lambda i, at: (0, at[i], 0)),
        ),
        out_shape=jax.ShapeDtypeStruct((total, 4 * quarter, width), f32),
        compiler_params=limits(16),
        cost_estimate=cost(1e6, 32 * quarter * width),
        name="put",
    )(place, *flat)


def finish_kernel(steps, blocks_ref, inverse_ref, *refs):
    values, refs = refs[:4], refs[4:]
    coefficient_refs, upper_refs, refs = refs[:steps], refs[steps : 2 * steps], refs[2 * steps :]
    out_ref, diagonal_ref, factor_ref, held, sent = refs
    quarter, width = values[0].shape
    joined = jnp.concatenate(halves_of(inverse_ref[...].T), axis=1)
    right = jnp.concatenate([joined, joined], axis=0)
    copies = []
    for at, place in enumerate(quarter_places()):
        left = jnp.concatenate(halves_of(values[at][...]), axis=1)
        sums = product(left, right)
        held[at] = sums[:, :width] + sums[:, width:]
        rows = pl.ds(pl.multiple_of(place * quarter, quarter), quarter)
        copies.append(pltpu.make_async_copy(held.at[at], out_ref.at[steps - 1, rows], sent.at[at]))
        copies[-1].start()
    for at in range(steps):
        diagonal_ref[at] = coefficient_refs[at][:, -width:].T
        factor_ref[at] = upper_refs[at][...]
    for copy in copies:
        copy.wait()


def finish(blocks, inverse, values, coefficients_list, uppers):
    quarter, width = values[0].shape
    steps = len(uppers)
    small = jax.ShapeDtypeStruct((steps, width, width), f32)
    return pl.pallas_call(
        functools.partial(finish_kernel, steps),
        in_specs=[pl.BlockSpec(memory_space=pl.ANY)] + in_vmem(5 + 2 * steps),
        out_specs=[pl.BlockSpec(memory_space=pl.ANY)] + in_vmem(2),
        out_shape=[jax.ShapeDtypeStruct(blocks.shape, f32), small, small],
        scratch_shapes=[pltpu.VMEM((4, quarter, width), f32), pltpu.SemaphoreType.DMA((4,))],
        input_output_aliases={0: 0},
        compiler_params=limits(16),
        cost_estimate=cost(32 * quarter * width * width, 48 * quarter * width),
        name="finish",
    )(blocks, inverse, *values, *coefficients_list, *uppers)


def along_rows(value, by):
    length = lax.axis_size("rows")
    return lax.ppermute(value, "rows", [(i, (i + by) % length) for i in range(length)])


def across(value, bit):
    return lax.ppermute(value, "basis", [(i, i ^ bit) for i in range(lax.axis_size("basis"))])


def spread_kernel(nodes, taken_ref, out_ref):
    total = taken_ref[0]
    for at in range(1, taken_ref.shape[0]):
        total = total + taken_ref[at]
    total = total / nodes
    for at in range(out_ref.shape[0]):
        out_ref[at] = total


def summed(value, axes, nodes):
    rows, columns = value.shape
    devices = 1
    for axis in axes:
        devices *= lax.axis_size(axis)
    if rows % devices:
        return lax.psum(value, axes) / nodes
    pieces = value.reshape(devices, rows // devices, columns)
    taken = lax.all_to_all(pieces, axes, 0, 0, tiled=True)
    spread = pl.pallas_call(
        functools.partial(spread_kernel, nodes),
        in_specs=in_vmem(1),
        out_specs=in_vmem(1)[0],
        out_shape=jax.ShapeDtypeStruct(pieces.shape, f32),
        compiler_params=limits(8),
        cost_estimate=cost(pieces.size, 8 * pieces.size),
        name="spread",
    )(taken)
    return lax.all_to_all(spread, axes, 0, 0, tiled=True).reshape(rows, columns)


def local(tiles, tile_pairs, degree, start_block, stored):
    rows_count = lax.axis_size("rows")
    rows_index = lax.axis_index("rows")
    local_rows, width = start_block.shape
    first_fresh = stored.shape[0] * width
    quarter = local_rows // 4
    blocks_here = local_rows // tiles.shape[1]
    all_nodes = local_rows * rows_count
    all_blocks = blocks_here * rows_count
    row_local = tile_pairs[:, 0] - rows_index * blocks_here
    column_local = jnp.mod(tile_pairs[:, 1] - (rows_index - REACH) * blocks_here, all_blocks)
    row_scale = jnp.broadcast_to((1.0 / jnp.sqrt(degree.astype(f32)))[:, None], start_block.shape)
    places = quarter_places()

    def quarters_of(value):
        return [lax.dynamic_slice_in_dim(value, place * quarter, quarter, 0) for place in places]

    current = quarters_of(start_block)
    scaled = [(scale * block).astype(bf16) for scale, block in zip(quarters_of(row_scale), current)]
    scales = quarters_of(row_scale)
    scale_half = jnp.concatenate(scales[:2])
    fresh = [current]
    coefficients_list, factor_list = ([], [])
    blocks = None
    for iteration in range(ITERS):
        last = iteration == ITERS - 1
        pieces = {0: [scaled[:2], scaled[2:]]}
        for distance in range(REACH, 0, -1):
            for by in (-distance, distance):
                if distance > 1:
                    own = along_rows(scaled[0], -by)
                    mine = [own, across(own, CHIP_BIT)]
                else:
                    mine = [along_rows(jnp.concatenate(scaled[:2]), -by)]
                pieces[by] = [mine, [across(piece, CORE_BIT) for piece in mine]]
        if last:
            blocks = put(jnp.stack(places), fresh[1:], ITERS)
            row_local, blocks = lax.optimization_barrier((row_local, blocks))
        ranges = [by + REACH for by in pieces]
        sources = list(pieces.values())
        keep, send = tile_products(tiles, row_local, column_local, ranges, sources)
        here = keep + across(send, CORE_BIT)
        there = across(here, CHIP_BIT)
        image = here + jnp.concatenate([there[quarter:], there[:quarter]])
        lifted = jnp.concatenate(current[:2]) - scale_half * image
        lifted_other = across(lifted, CORE_BIT)
        part = coefficients((0, 1), lifted, stored, fresh, None)
        part = coefficients((2, 3), lifted_other, stored, fresh, part)
        lifted_own = lifted[:quarter]
        coefficient = summed(part, ("rows",), all_nodes)
        term_cross, term_far = correction((3, 1), stored, coefficient)
        term_near, term_own = correction((2, 0), stored, coefficient)
        far_sum = across(term_far + across(term_cross, CORE_BIT), CHIP_BIT)
        near_sum = across(term_near, CORE_BIT)
        remainder, gram_part = remainder_part(
            lifted_own, term_own, near_sum, far_sum, coefficient, [block[0] for block in fresh], first_fresh
        )
        remainder_near = across(remainder, CORE_BIT)
        remainder_far = across(remainder, CHIP_BIT)
        gram = summed(gram_part, ("rows", "basis"), all_nodes)
        remainder_far, _ = lax.optimization_barrier((remainder_far, gram))
        remainder_cross = across(remainder_far, CORE_BIT)
        upper, inverse = factor(gram)
        coefficients_list.append(coefficient)
        factor_list.append(upper)
        values = [remainder, remainder_far, remainder_near, remainder_cross]
        if last:
            return tuple(finish(blocks, inverse, values, coefficients_list, factor_list))
        current, scaled = solve(inverse, values, scales)
        fresh.append(current)


def solution(mesh):
    placed = (
        P(("rows", "basis"), None, None),
        P(("rows", "basis"), None),
        P("rows"),
        P("rows", None),
        P("basis", "rows", None),
    )
    return jax.shard_map(
        local,
        mesh=mesh,
        in_specs=placed,
        out_specs=(P(None, "rows", None), P(), P()),
        check_vma=False,
    )
```

time: 899 us -> 342 us (0.38)
  waiting for transfers between devices: 592 us -> 152 us
  matrix products: 130 us -> 0 us
  blocking collectives: 0 us -> 91.5 us
  local copies, waits for them, and re-layouts: 81.5 us -> 11.8 us
  other arithmetic: 56.1 us -> 4.56 us
  Pallas kernels: 0 us -> 46.5 us
  starting transfers between devices: 15.7 us -> 33.4 us
  between operations: 15 us -> 1.3 us
    psum x8 -> x0, waiting for transfers between devices: 485 us -> none  [the longest x2 144 us: local(): stored_coef, fresh_coef = lax.psum((stored_part, fresh_part), 'rows')]
    dot_general x14 -> x0, matrix products: 123 us -> none  [the longest x2 30.8 us: local(): jnp.einsum('tij,tjc->tic', tiles, chosen, preferred_element_type=jnp.floa...]
    ppermute x8 -> x42, waiting for transfers between devices: 27.7 us -> 138 us  [the longest x34 97.1 us: across(): lax.ppermute(value, 'basis', [(i, i ^ bit) for i in range(lax.axis_size('...]
    all_to_all x0 -> x6, blocking collectives: none -> 91.5 us  [the longest x4 62.8 us: summed(): taken = lax.all_to_all(pieces, axes, 0, 0, tiled=True)]
    all_gather x2 -> x0, waiting for transfers between devices: 79.5 us -> none  [local(): lax.all_gather(neighbour_range(column_part), 'basis', axis=1, tiled=True)]
    another operation x13 -> x1, other arithmetic: 48 us -> 0.08 us  [local(): blocks = put(jnp.stack(places), fresh[1:], ITERS)]
    pallas_call x0 -> x21, Pallas kernels: none -> 46.5 us  [the longest x2 13.4 us: tile_products(): pl.pallas_call(functools.partial(tile_kernel, step_tiles, targets), in_sp...]
    reshape x6 -> x0, local copies, waits for them, and re-layouts: 27.4 us -> none  [the longest x2 16.2 us: local(): tile_grid = extended.reshape(-1, tile_width, block_width)]
  transfers between devices with their start and end apart: 18 -> 44, of which waited for: 16 -> 20; matrix products, arithmetic and copies ran while one was open for 0% -> 0% of each run, Pallas kernels for 0% -> 5%
where the time goes in v2:
time: 342 us; the launch traced here: 341 us
  waiting for transfers between devices  152 us (44%)
  blocking collectives  91.5 us (27%)
  Pallas kernels  46.5 us (14%)
  starting transfers between devices  33.4 us (10%)
  local copies, waits for them, and re-layouts  11.8 us (3%)
  other arithmetic  4.56 us (1%)
    ppermute x34, waiting for transfers between devices, across(): lax.ppermute(value, 'basis', [(i, i ^ bit) for i in range(lax.axis_size('...  97.1 us
    all_to_all x4, blocking collectives, summed(): taken = lax.all_to_all(pieces, axes, 0, 0, tiled=True)  62.8 us
    ppermute x8, waiting for transfers between devices, along_rows(): lax.ppermute(value, 'rows', [(i, (i + by) % length) for i in range(length)])  40.8 us
    all_to_all x2, blocking collectives, summed(): return lax.all_to_all(spread, axes, 0, 0, tiled=True).reshape(rows, columns)  28.6 us
    ppermute x34, starting transfers between devices, across(): lax.ppermute(value, 'basis', [(i, i ^ bit) for i in range(lax.axis_size('...  15.2 us
    all_to_all x2, waiting for transfers between devices, summed(): return lax.all_to_all(spread, axes, 0, 0, tiled=True).reshape(rows, columns)  14.3 us
    pallas_call x2, Pallas kernels, tile_products(): pl.pallas_call(functools.partial(tile_kernel, step_tiles, targets), in_sp...  13.4 us
    ppermute x8, starting transfers between devices, along_rows(): lax.ppermute(value, 'rows', [(i, (i + by) % length) for i in range(length)])  12.2 us
  transfers between devices with their start and end apart: 44, of which 20 were waited for; matrix products, arithmetic and copies ran while one was open for 0% of the time, Pallas kernels for 5%

profile of v2, /device:TPU:0, one launch (start us, length us, event | category | flops | bytes accessed | tf_op | source)
XLA Modules:
  0.0 341.2 jit_solution(6944120470904473672)
XLA Ops:
  4.1 6.1 %collective-permute-start.10 = (bf16[2048,128]{1,0:T(8,128)(2,1)S(1)}, bf16[2048,128]{1,0:T(8,128)(2,1)S(1)}, u32[]{:S(2)}, u32[]{:S(2)}) collective-permute-start(bf16[2048,128]{1,0:T(8,128)(2,1)S(1)} %pad_maximum_fusion.1), channel_id=1, source_target_pairs={{0,28},{4,0},{8,4},{12,8},{16,12},{20,16},{24,20},{28,24},{1,29},{... | collective-permute-start | bytes 1572872 | tf_op jit(solution)/shard_map/ppermute | solution.py:381
  12.3 15.9 %collective-permute-done.4.refs_8_ = bf16[1024,128]{1,0:T(8,128)(2,1)} collective-permute-done((bf16[1024,128]{1,0:T(8,128)(2,1)S(1)}, bf16[1024,128]{1,0:T(8,128)(2,1)}, u32[]{:S(2)}, u32[]{:S(2)}) %collective-permute-start.4) | collective-permute-done | bytes 262176 | tf_op jit(solution)/shard_map/ppermute | solution.py:381
  29.7 4.0 %collective-permute-done.refs_4_ = bf16[1024,128]{1,0:T(8,128)(2,1)} collective-permute-done((bf16[1024,128]{1,0:T(8,128)(2,1)S(1)}, bf16[1024,128]{1,0:T(8,128)(2,1)}, u32[]{:S(2)}, u32[]{:S(2)}) %collective-permute-start) | collective-permute-done | bytes 262176 | tf_op jit(solution)/shard_map/ppermute | solution.py:381
  37.7 5.2 %collective-permute-done.1.refs_5_ = bf16[1024,128]{1,0:T(8,128)(2,1)} collective-permute-done((bf16[1024,128]{1,0:T(8,128)(2,1)}, bf16[1024,128]{1,0:T(8,128)(2,1)}, u32[]{:S(2)}, u32[]{:S(2)}) %collective-permute-start.1) | collective-permute-done | bytes 262176 | tf_op jit(solution)/shard_map/ppermute | solution.py:385
  44.8 4.1 %copy-done = bf16[80,256,256]{2,1,0:T(8,128)(2,1)S(1)} copy-done((bf16[80,256,256]{2,1,0:T(8,128)(2,1)S(1)}, bf16[80,256,256]{2,1,0:T(8,128)(2,1)}, u32[]{:S(2)}) %copy-start) | copy-done | bytes 10485784
  49.9 7.6 %tile_products.2 = (f32[2048,128]{1,0:T(8,128)S(1)}, f32[2048,128]{1,0:T(8,128)S(1)}) custom-call(s32[80]{0:T(128)S(1)} %subtract_bitcast_fusion.row_ref, s32[80]{0:T(128)S(1)} %and_select_fusion.column_ref, bf16[80,256,256]{2,1,0:T(8,128)(2,1)S(1)} %copy-done, bf16[1024,128]{1,0:T(8,128)(2,1)S(1)} %get-tuple-element.77.refs_0_, ...), custom_call_target="tpu_custom_call" | custom-call | flops 1342177280 | bytes 10485760 | tf_op jit(solution)/shard_map/tile_products/pallas_call | solution.py:101
  62.0 23.7 %collective-permute-done.13 = f32[2048,128]{1,0:T(8,128)S(1)} collective-permute-done((f32[2048,128]{1,0:T(8,128)S(1)}, f32[2048,128]{1,0:T(8,128)S(1)}, u32[]{:S(2)}, u32[]{:S(2)}) %collective-permute-start.13) | collective-permute-done | bytes 1048608 | tf_op jit(solution)/shard_map/ppermute | solution.py:385
  91.1 18.1 %all_to_all.40.taken_ref = f32[8,16,640]{2,1,0:T(8,128)S(1)} all-to-all(f32[8,16,640]{2,1,0:T(8,128)S(1)} %bitcast.29), channel_id=1, replica_groups=mesh['rows'=8,'basis'=4] {'rows'}, dimensions={0} | all-to-all | bytes 655360 | tf_op jit(solution)/shard_map/all_to_all | solution.py:405
  109.3 13.6 %all_to_all.41 = f32[8,16,640]{2,1,0:T(8,128)S(1)} all-to-all(f32[8,16,640]{2,1,0:T(8,128)S(1)} %spread.4), channel_id=1, replica_groups=mesh['rows'=8,'basis'=4] {'rows'}, dimensions={0} | all-to-all | bytes 655360 | tf_op jit(solution)/shard_map/all_to_all | solution.py:415
  127.9 12.4 %collective-permute-done.17.far_ref = f32[1024,128]{1,0:T(8,128)S(1)} collective-permute-done((f32[1024,128]{1,0:T(8,128)S(1)}, f32[1024,128]{1,0:T(8,128)S(1)}, u32[]{:S(2)}, u32[]{:S(2)}) %collective-permute-start.17) | collective-permute-done | bytes 524320 | tf_op jit(solution)/shard_map/ppermute | solution.py:385
  143.8 12.8 %all_to_all.42.taken_ref = f32[32,4,128]{2,1,0:T(4,128)S(1)} all-to-all(f32[32,4,128]{2,1,0:T(4,128)S(1)} %bitcast.33), channel_id=1, replica_groups=mesh['rows'=8,'basis'=4] {'rows','basis'}, dimensions={0} | all-to-all | bytes 131072 | tf_op jit(solution)/shard_map/all_to_all | solution.py:405
  160.9 7.1 %all-to-all-done.3 = f32[32,4,128]{2,1,0:T(4,128)S(1)} async-done(((f32[32,4,128]{2,1,0:T(4,128)}), f32[32,4,128]{2,1,0:T(4,128)S(1)}, u32[]{:S(2)}, u32[]{:S(2)}) %all-to-all-start.3) | async-done | bytes 65568 | tf_op jit(solution)/shard_map/all_to_all | solution.py:415
  169.6 4.0 %factor.2 = (f32[128,128]{1,0:T(8,128)S(1)}, f32[128,128]{1,0:T(8,128)S(1)}) custom-call(f32[128,128]{1,0:T(8,128)S(1)} %bitcast.30), custom_call_target="tpu_custom_call" | custom-call | flops 200000000 | bytes 65536 | tf_op jit(solution)/shard_map/factor/pallas_call | solution.py:273
  180.3 16.3 %collective-permute-done.25.refs_8_ = bf16[1024,128]{1,0:T(8,128)(2,1)S(1)} collective-permute-done((bf16[1024,128]{1,0:T(8,128)(2,1)S(1)}, bf16[1024,128]{1,0:T(8,128)(2,1)S(1)}, u32[]{:S(2)}, u32[]{:S(2)}) %collective-permute-start.25) | collective-permute-done | bytes 262176 | tf_op jit(solution)/shard_map/ppermute | solution.py:381
  197.4 4.5 %collective-permute-done.21.refs_4_ = bf16[1024,128]{1,0:T(8,128)(2,1)S(1)} collective-permute-done((bf16[1024,128]{1,0:T(8,128)(2,1)S(1)}, bf16[1024,128]{1,0:T(8,128)(2,1)S(1)}, u32[]{:S(2)}, u32[]{:S(2)}) %collective-permute-start.21) | collective-permute-done | bytes 262176 | tf_op jit(solution)/shard_map/ppermute | solution.py:381
  205.8 5.2 %collective-permute-done.22.refs_5_ = bf16[1024,128]{1,0:T(8,128)(2,1)S(1)} collective-permute-done((bf16[1024,128]{1,0:T(8,128)(2,1)S(1)}, bf16[1024,128]{1,0:T(8,128)(2,1)S(1)}, u32[]{:S(2)}, u32[]{:S(2)}) %collective-permute-start.22) | collective-permute-done | bytes 262176 | tf_op jit(solution)/shard_map/ppermute | solution.py:385
  213.5 4.1 %copy-done.1 = bf16[80,256,256]{2,1,0:T(8,128)(2,1)S(1)} copy-done((bf16[80,256,256]{2,1,0:T(8,128)(2,1)S(1)}, bf16[80,256,256]{2,1,0:T(8,128)(2,1)}, u32[]{:S(2)}) %copy-start.1) | copy-done | bytes 10485784
  217.6 5.8 %tile_products.3 = (f32[2048,128]{1,0:T(8,128)S(1)}, f32[2048,128]{1,0:T(8,128)S(1)}) custom-call(s32[80]{0:T(128)S(1)} %subtract_bitcast_fusion.row_ref, s32[80]{0:T(128)S(1)} %and_select_fusion.column_ref, bf16[80,256,256]{2,1,0:T(8,128)(2,1)S(1)} %copy-done.1, bf16[1024,128]{1,0:T(8,128)(2,1)S(1)} %get-tuple-element.51.refs_0_, ...), custom_call_target="tpu_custom_call" | custom-call | flops 1342177280 | bytes 10485760 | tf_op jit(solution)/shard_map/tile_products/pallas_call | solution.py:101
  227.2 24.7 %collective-permute-done.34 = f32[2048,128]{1,0:T(8,128)S(1)} collective-permute-done((f32[2048,128]{1,0:T(8,128)S(1)}, f32[2048,128]{1,0:T(8,128)S(1)}, u32[]{:S(2)}, u32[]{:S(2)}) %collective-permute-start.34) | collective-permute-done | bytes 1048608 | tf_op jit(solution)/shard_map/ppermute | solution.py:385
  256.9 18.3 %all_to_all.43.taken_ref = f32[8,16,768]{2,1,0:T(8,128)S(1)} all-to-all(f32[8,16,768]{2,1,0:T(8,128)S(1)} %bitcast.28), channel_id=1, replica_groups=mesh['rows'=8,'basis'=4] {'rows'}, dimensions={0} | all-to-all | bytes 786432 | tf_op jit(solution)/shard_map/all_to_all | solution.py:405
  275.2 15.0 %all_to_all.44 = f32[8,16,768]{2,1,0:T(8,128)S(1)} all-to-all(f32[8,16,768]{2,1,0:T(8,128)S(1)} %spread.6), channel_id=1, replica_groups=mesh['rows'=8,'basis'=4] {'rows'}, dimensions={0} | all-to-all | bytes 786432 | tf_op jit(solution)/shard_map/all_to_all | solution.py:415
  295.1 12.5 %collective-permute-done.38.far_ref = f32[1024,128]{1,0:T(8,128)S(1)} collective-permute-done((f32[1024,128]{1,0:T(8,128)S(1)}, f32[1024,128]{1,0:T(8,128)S(1)}, u32[]{:S(2)}, u32[]{:S(2)}) %collective-permute-start.38) | collective-permute-done | bytes 524320 | tf_op jit(solution)/shard_map/ppermute | solution.py:385
  310.0 13.7 %all_to_all.45.taken_ref = f32[32,4,128]{2,1,0:T(4,128)S(1)} all-to-all(f32[32,4,128]{2,1,0:T(4,128)S(1)} %bitcast.32), channel_id=1, replica_groups=mesh['rows'=8,'basis'=4] {'rows','basis'}, dimensions={0} | all-to-all | bytes 131072 | tf_op jit(solution)/shard_map/all_to_all | solution.py:405
  327.1 7.2 %all-to-all-done.7 = f32[32,4,128]{2,1,0:T(4,128)S(1)} async-done(((f32[32,4,128]{2,1,0:T(4,128)}), f32[32,4,128]{2,1,0:T(4,128)S(1)}, u32[]{:S(2)}, u32[]{:S(2)}) %all-to-all-start.7) | async-done | bytes 65568 | tf_op jit(solution)/shard_map/all_to_all | solution.py:415
  (136 shorter events, 78.0 us)
Async XLA Ops:
  4.1 31.1 %collective-permute-start.10 = (bf16[2048,128]{1,0:T(8,128)(2,1)S(1)}, bf16[2048,128]{1,0:T(8,128)(2,1)S(1)}, u32[]{:S(2)}, u32[]{:S(2)}) collective-permute-start(bf16[2048,128]{1,0:T(8,128)(2,1)S(1)} %pad_maximum_fusion.1), channel_id=1, source_target_pairs={{0,28},{4,0},{8,4},{12,8},{16,12},{20,16},{24,20},{28,24},{1,29},{... | collective-permute-start | bytes 1572872 | tf_op jit(solution)/shard_map/ppermute | solution.py:381
  10.2 25.0 %collective-permute-start.8 = (bf16[2048,128]{1,0:T(8,128)(2,1)S(1)}, bf16[2048,128]{1,0:T(8,128)(2,1)}, u32[]{:S(2)}, u32[]{:S(2)}) collective-permute-start(bf16[2048,128]{1,0:T(8,128)(2,1)S(1)} %pad_maximum_fusion.1), channel_id=1, source_target_pairs={{0,4},{4,8},{8,12},{12,16},{16,20},{20,24},{24,28},{28,0},{1,5},{5... | collective-permute-start | bytes 1572872 | tf_op jit(solution)/shard_map/ppermute | solution.py:381
  10.2 18.0 %collective-permute-start.4 = (bf16[1024,128]{1,0:T(8,128)(2,1)S(1)}, bf16[1024,128]{1,0:T(8,128)(2,1)}, u32[]{:S(2)}, u32[]{:S(2)}) collective-permute-start(bf16[1024,128]{1,0:T(8,128)(2,1)S(1)} %get-tuple-element.77.refs_0_), channel_id=1, source_target_pairs={{0,24},{4,28},{8,0},{12,4},{16,8},{20,12},{24,16},{28,20},{1,25},{... | collective-permute-start | bytes 786440 | tf_op jit(solution)/shard_map/ppermute | solution.py:381
  11.3 22.4 %collective-permute-start = (bf16[1024,128]{1,0:T(8,128)(2,1)S(1)}, bf16[1024,128]{1,0:T(8,128)(2,1)}, u32[]{:S(2)}, u32[]{:S(2)}) collective-permute-start(bf16[1024,128]{1,0:T(8,128)(2,1)S(1)} %get-tuple-element.77.refs_0_), channel_id=1, source_target_pairs={{0,8},{4,12},{8,16},{12,20},{16,24},{20,28},{24,0},{28,4},{1,9},{5... | collective-permute-start | bytes 786440 | tf_op jit(solution)/shard_map/ppermute | solution.py:381
  28.2 9.5 %collective-permute-start.5 = (bf16[1024,128]{1,0:T(8,128)(2,1)}, bf16[1024,128]{1,0:T(8,128)(2,1)}, u32[]{:S(2)}, u32[]{:S(2)}) collective-permute-start(bf16[1024,128]{1,0:T(8,128)(2,1)} %collective-permute-done.4.refs_8_), channel_id=1, source_target_pairs={{0,2},{1,3},{2,0},{3,1},{4,6},{5,7},{6,4},{7,5},{8,10},{9,11},{10,... | collective-permute-start | bytes 786440 | tf_op jit(solution)/shard_map/ppermute | solution.py:385
  35.2 9.5 %collective-permute-start.11 = (bf16[2048,128]{1,0:T(8,128)(2,1)S(1)}, bf16[2048,128]{1,0:T(8,128)(2,1)}, u32[]{:S(2)}, u32[]{:S(2)}) collective-permute-start(bf16[2048,128]{1,0:T(8,128)(2,1)S(1)} %collective-permute-done.10.refs_16_.refs_17_), channel_id=1, source_target_pairs={{0,1},{1,0},{2,3},{3,2},{4,5},{5,4},{6,7},{7,6},{8,9},{9,8},{10,11... | collective-permute-start | bytes 1572872 | tf_op jit(solution)/shard_map/ppermute | solution.py:385
  35.2 9.5 %collective-permute-start.9 = (bf16[2048,128]{1,0:T(8,128)(2,1)}, bf16[2048,128]{1,0:T(8,128)(2,1)}, u32[]{:S(2)}, u32[]{:S(2)}) collective-permute-start(bf16[2048,128]{1,0:T(8,128)(2,1)} %collective-permute-done.8.refs_12_.refs_13_), channel_id=1, source_target_pairs={{0,1},{1,0},{2,3},{3,2},{4,5},{5,4},{6,7},{7,6},{8,9},{9,8},{10,11... | collective-permute-start | bytes 1572872 | tf_op jit(solution)/shard_map/ppermute | solution.py:385
  60.4 25.3 %collective-permute-start.13 = (f32[2048,128]{1,0:T(8,128)S(1)}, f32[2048,128]{1,0:T(8,128)S(1)}, u32[]{:S(2)}, u32[]{:S(2)}) collective-permute-start(f32[2048,128]{1,0:T(8,128)S(1)} %add.67), channel_id=1, source_target_pairs={{0,2},{1,3},{2,0},{3,1},{4,6},{5,7},{6,4},{7,5},{8,10},{9,11},{10,... | collective-permute-start | bytes 3145736 | tf_op jit(solution)/shard_map/ppermute | solution.py:385
  126.3 14.0 %collective-permute-start.17 = (f32[1024,128]{1,0:T(8,128)S(1)}, f32[1024,128]{1,0:T(8,128)S(1)}, u32[]{:S(2)}, u32[]{:S(2)}) collective-permute-start(f32[1024,128]{1,0:T(8,128)S(1)} %add.69), channel_id=1, source_target_pairs={{0,2},{1,3},{2,0},{3,1},{4,6},{5,7},{6,4},{7,5},{8,10},{9,11},{10,... | collective-permute-start | bytes 1572872 | tf_op jit(solution)/shard_map/ppermute | solution.py:385
  142.2 26.3 %collective-permute-start.18 = (f32[1024,128]{1,0:T(8,128)}, f32[1024,128]{1,0:T(8,128)}, u32[]{:S(2)}, u32[]{:S(2)}) collective-permute-start(f32[1024,128]{1,0:T(8,128)} %get-tuple-element.43.refs_0_), channel_id=1, source_target_pairs={{0,2},{1,3},{2,0},{3,1},{4,6},{5,7},{6,4},{7,5},{8,10},{9,11},{10,... | collective-permute-start | bytes 1572872 | tf_op jit(solution)/shard_map/ppermute | solution.py:385
  157.2 10.7 %all-to-all-start.3 = ((f32[32,4,128]{2,1,0:T(4,128)}), f32[32,4,128]{2,1,0:T(4,128)S(1)}, u32[]{:S(2)}, u32[]{:S(2)}) async-start(f32[32,4,128]{2,1,0:T(4,128)} %spread.5), calls=%async_computation.3 | async-start | bytes 131072 | tf_op jit(solution)/shard_map/all_to_all | solution.py:415
  160.7 12.8 %collective-permute-start.19 = (f32[1024,128]{1,0:T(8,128)}, f32[1024,128]{1,0:T(8,128)}, u32[]{:S(2)}, u32[]{:S(2)}) collective-permute-start(f32[1024,128]{1,0:T(8,128)} %get-tuple-element.43.refs_0_), channel_id=1, source_target_pairs={{0,1},{1,0},{2,3},{3,2},{4,5},{5,4},{6,7},{7,6},{8,9},{9,8},{10,11... | collective-permute-start | bytes 1572872 | tf_op jit(solution)/shard_map/ppermute | solution.py:385
  176.2 26.3 %collective-permute-start.31 = (bf16[2048,128]{1,0:T(8,128)(2,1)S(1)}, bf16[2048,128]{1,0:T(8,128)(2,1)S(1)}, u32[]{:S(2)}, u32[]{:S(2)}) collective-permute-start(bf16[2048,128]{1,0:T(8,128)(2,1)S(1)} %constant_dynamic-update-slice_fusion), channel_id=1, source_target_pairs={{0,28},{4,0},{8,4},{12,8},{16,12},{20,16},{24,20},{28,24},{1,29},{... | collective-permute-start | bytes 1572872 | tf_op jit(solution)/shard_map/ppermute | solution.py:381
  177.1 25.4 %collective-permute-start.29 = (bf16[2048,128]{1,0:T(8,128)(2,1)S(1)}, bf16[2048,128]{1,0:T(8,128)(2,1)S(1)}, u32[]{:S(2)}, u32[]{:S(2)}) collective-permute-start(bf16[2048,128]{1,0:T(8,128)(2,1)S(1)} %constant_dynamic-update-slice_fusion), channel_id=1, source_target_pairs={{0,4},{4,8},{8,12},{12,16},{16,20},{20,24},{24,28},{28,0},{1,5},{5... | collective-permute-start | bytes 1572872 | tf_op jit(solution)/shard_map/ppermute | solution.py:381
  178.3 18.3 %collective-permute-start.25 = (bf16[1024,128]{1,0:T(8,128)(2,1)S(1)}, bf16[1024,128]{1,0:T(8,128)(2,1)S(1)}, u32[]{:S(2)}, u32[]{:S(2)}) collective-permute-start(bf16[1024,128]{1,0:T(8,128)(2,1)S(1)} %get-tuple-element.51.refs_0_), channel_id=1, source_target_pairs={{0,24},{4,28},{8,0},{12,4},{16,8},{20,12},{24,16},{28,20},{1,25},{... | collective-permute-start | bytes 786440 | tf_op jit(solution)/shard_map/ppermute | solution.py:381
  179.1 22.8 %collective-permute-start.21 = (bf16[1024,128]{1,0:T(8,128)(2,1)S(1)}, bf16[1024,128]{1,0:T(8,128)(2,1)S(1)}, u32[]{:S(2)}, u32[]{:S(2)}) collective-permute-start(bf16[1024,128]{1,0:T(8,128)(2,1)S(1)} %get-tuple-element.51.refs_0_), channel_id=1, source_target_pairs={{0,8},{4,12},{8,16},{12,20},{16,24},{20,28},{24,0},{28,4},{1,9},{5... | collective-permute-start | bytes 786440 | tf_op jit(solution)/shard_map/ppermute | solution.py:381
  202.6 10.9 %collective-permute-start.32 = (bf16[2048,128]{1,0:T(8,128)(2,1)S(1)}, bf16[2048,128]{1,0:T(8,128)(2,1)S(1)}, u32[]{:S(2)}, u32[]{:S(2)}) collective-permute-start(bf16[2048,128]{1,0:T(8,128)(2,1)S(1)} %collective-permute-done.31.refs_16_.refs_17_), channel_id=1, source_target_pairs={{0,1},{1,0},{2,3},{3,2},{4,5},{5,4},{6,7},{7,6},{8,9},{9,8},{10,11... | collective-permute-start | bytes 1572872 | tf_op jit(solution)/shard_map/ppermute | solution.py:385
  202.6 10.9 %collective-permute-start.30 = (bf16[2048,128]{1,0:T(8,128)(2,1)S(1)}, bf16[2048,128]{1,0:T(8,128)(2,1)S(1)}, u32[]{:S(2)}, u32[]{:S(2)}) collective-permute-start(bf16[2048,128]{1,0:T(8,128)(2,1)S(1)} %collective-permute-done.29.refs_12_.refs_13_), channel_id=1, source_target_pairs={{0,1},{1,0},{2,3},{3,2},{4,5},{5,4},{6,7},{7,6},{8,9},{9,8},{10,11... | collective-permute-start | bytes 1572872 | tf_op jit(solution)/shard_map/ppermute | solution.py:385
  203.1 10.4 %collective-permute-start.23 = (bf16[1024,128]{1,0:T(8,128)(2,1)S(1)}, bf16[1024,128]{1,0:T(8,128)(2,1)S(1)}, u32[]{:S(2)}, u32[]{:S(2)}) collective-permute-start(bf16[1024,128]{1,0:T(8,128)(2,1)S(1)} %collective-permute-done.21.refs_4_), channel_id=1, source_target_pairs={{0,1},{1,0},{2,3},{3,2},{4,5},{5,4},{6,7},{7,6},{8,9},{9,8},{10,11... | collective-permute-start | bytes 786440 | tf_op jit(solution)/shard_map/ppermute | solution.py:385
  226.4 25.5 %collective-permute-start.34 = (f32[2048,128]{1,0:T(8,128)S(1)}, f32[2048,128]{1,0:T(8,128)S(1)}, u32[]{:S(2)}, u32[]{:S(2)}) collective-permute-start(f32[2048,128]{1,0:T(8,128)S(1)} %add.70), channel_id=1, source_target_pairs={{0,2},{1,3},{2,0},{3,1},{4,6},{5,7},{6,4},{7,5},{8,10},{9,11},{10,... | collective-permute-start | bytes 3145736 | tf_op jit(solution)/shard_map/ppermute | solution.py:385
  293.6 14.0 %collective-permute-start.38 = (f32[1024,128]{1,0:T(8,128)S(1)}, f32[1024,128]{1,0:T(8,128)S(1)}, u32[]{:S(2)}, u32[]{:S(2)}) collective-permute-start(f32[1024,128]{1,0:T(8,128)S(1)} %add.72), channel_id=1, source_target_pairs={{0,2},{1,3},{2,0},{3,1},{4,6},{5,7},{6,4},{7,5},{8,10},{9,11},{10,... | collective-permute-start | bytes 1572872 | tf_op jit(solution)/shard_map/ppermute | solution.py:385
  309.3 25.0 %collective-permute-start.39 = (f32[1024,128]{1,0:T(8,128)S(1)}, f32[1024,128]{1,0:T(8,128)S(1)}, u32[]{:S(2)}, u32[]{:S(2)}) collective-permute-start(f32[1024,128]{1,0:T(8,128)S(1)} %get-tuple-element.63.refs_0_), channel_id=1, source_target_pairs={{0,2},{1,3},{2,0},{3,1},{4,6},{5,7},{6,4},{7,5},{8,10},{9,11},{10,... | collective-permute-start | bytes 1572872 | tf_op jit(solution)/shard_map/ppermute | solution.py:385
  324.3 10.0 %all-to-all-start.7 = ((f32[32,4,128]{2,1,0:T(4,128)}), f32[32,4,128]{2,1,0:T(4,128)S(1)}, u32[]{:S(2)}, u32[]{:S(2)}) async-start(f32[32,4,128]{2,1,0:T(4,128)} %spread.7), calls=%async_computation.7 | async-start | bytes 131072 | tf_op jit(solution)/shard_map/all_to_all | solution.py:415
  326.9 11.5 %collective-permute-start.40 = (f32[1024,128]{1,0:T(8,128)S(1)}, f32[1024,128]{1,0:T(8,128)S(1)}, u32[]{:S(2)}, u32[]{:S(2)}) collective-permute-start(f32[1024,128]{1,0:T(8,128)S(1)} %get-tuple-element.63.refs_0_), channel_id=1, source_target_pairs={{0,1},{1,0},{2,3},{3,2},{4,5},{5,4},{6,7},{7,6},{8,9},{9,8},{10,11... | collective-permute-start | bytes 1572872 | tf_op jit(solution)/shard_map/ppermute | solution.py:385
  (30 other events, 299.4 us)
